TPU v7x, 512 devices: a whole 4x4x16 slice. The times are simulated.
512 devices in a mesh: dp: 16 (over y, z_hi, core), mp: 32 (over z_lo, x).
Axes of the slice: x: 4, y: 4, z: 16 (z_hi: 2, z_lo: 8; z = z_hi * 8 + z_lo), core: 2. Of those that a mesh axis runs over, the one named last changes fastest.
Arguments:
- grads: bfloat16 [16, 16, 32, 256, 256], P('dp', None, 'mp'), may hold values from -18 to 18
- layer_map: int32 [512], replicated, may hold values from 0 to 31, never falling along the last dimension, each value on 1 to 32 neighbouring positions
Outputs:
- roots: float32 [16, 32, 256, 256], P(None, 'mp', 'dp')
Inputs may be any that keep to these rules, and one draw needn't show every extreme that they name: `layer_map`: layer numbers never fall along b; every layer 0 to 31 holds 1 to 32 blocks.
All inputs are finite; a program needn't handle non-finite values.
Results may differ from a plain program's by a relative error of at most 0.0003.
Values sent between devices are 32-bit elements; how exact they have to be, the bound alone decides.
No kernel may reach another device: no remote copies, remote signals or barrier semaphores. Data moves between devices by JAX's collectives and lax.ppermute only.
A program may use at most 64 MiB of HBM per device.

v0:
```python
import jax
import jax.numpy as jnp
from jax import lax
from jax.sharding import Mesh
from jax.sharding import PartitionSpec as P

ITERS = 8
DP = ("dp_0", "dp_1", "dp_2")
MP = ("mp_0", "mp_1")
DP_MP = ("dp_0", "dp_1", "dp_2", "mp_0", "mp_1")


def over_axes(array, axes):
    for axis in axes:
        array = lax.psum(array, axis)
    return array


def newton_root(stats, ridge, live):
    order = stats.shape[-1]
    identity = jnp.eye(order, dtype=jnp.float32)
    damped = jnp.where(live[:, None, None], stats + ridge[:, None, None] * identity, identity)
    frobenius = jnp.sqrt(jnp.sum(damped * damped, axis=(1, 2)))
    scaled = 2.5 / frobenius
    current = (scaled**0.25)[:, None, None] * identity
    coupled = scaled[:, None, None] * damped
    for _ in range(ITERS):
        factor = 1.25 * identity - 0.25 * coupled
        current = jnp.einsum("sij,sjk->sik", current, factor, precision=lax.Precision.HIGHEST)
        square = jnp.einsum("sij,sjk->sik", factor, factor, precision=lax.Precision.HIGHEST)
        fourth = jnp.einsum("sij,sjk->sik", square, square, precision=lax.Precision.HIGHEST)
        coupled = jnp.einsum("sij,sjk->sik", fourth, coupled, precision=lax.Precision.HIGHEST)
    return current


def local(grads, layer_map):
    gradient = grads[0, :, 0]
    blocks_here, order, columns = gradient.shape
    replicas = lax.axis_size(DP)
    holders = lax.axis_size(MP)
    band = order // replicas
    replica = lax.axis_index(DP)
    holder = lax.axis_index(MP)
    partial_value = jnp.einsum(
        "bic,bjc->bij", gradient, gradient, preferred_element_type=jnp.float32
    ) * (1.0 / (replicas * columns))
    mine = lax.psum_scatter(partial_value, DP, scatter_dimension=1, tiled=True)
    layer_grid = layer_map.reshape(blocks_here, holders)
    my_layers = lax.dynamic_slice_in_dim(layer_grid, holder, 1, 1)[:, 0]
    layer_ids = jnp.arange(holders, dtype=jnp.int32)
    local_onehot = (my_layers[:, None] == layer_ids[None, :]).astype(jnp.float32)
    all_counts = jnp.sum((layer_map[:, None] == layer_ids[None, :]).astype(jnp.int32), axis=0)
    diag_rows = lax.dynamic_slice_in_dim(mine, replica * band, band, 2)
    diag_part = jnp.trace(diag_rows, axis1=1, axis2=2)
    layer_part = jnp.dot(diag_part, local_onehot, precision=lax.Precision.HIGHEST)
    layer_total = over_axes(layer_part, DP_MP)
    layer_ridge = 0.1 * layer_total / (all_counts.astype(jnp.float32) * order)
    spread = -(-blocks_here // replicas)
    extra = replicas * spread - blocks_here
    stacked = lax.all_to_all(mine, DP, split_axis=0, concat_axis=1, tiled=True)
    block_ridge = jnp.pad(
        jnp.dot(local_onehot, layer_ridge, precision=lax.Precision.HIGHEST), (0, extra)
    )
    slot_ridge = lax.dynamic_slice_in_dim(block_ridge, replica * spread, spread, 0)
    slot_index = replica * spread + jnp.arange(spread, dtype=jnp.int32)
    solved = newton_root(stacked, slot_ridge, slot_index < blocks_here)
    returned = lax.all_to_all(solved, DP, split_axis=1, concat_axis=0, tiled=True)
    result = returned[:blocks_here]
    return result.reshape(blocks_here, 1, band, order)


def solution(mesh):
    torus = Mesh(mesh.devices.reshape(4, 2, 2, 8, 4), ("dp_0", "dp_1", "dp_2", "mp_0", "mp_1"))
    in_specs = (P(DP, None, MP, None, None), P())
    out_specs = P(None, MP, DP, None)
    return jax.shard_map(local, mesh=torus, in_specs=in_specs, out_specs=out_specs, check_vma=False)
```

profile of v0, /device:TPU:1, one launch (start us, length us, event | category | flops | bytes accessed | tf_op | source)
XLA Modules:
  0.0 299.2 jit_solution(11031274429104492397)
XLA Ops:
  6.5 1.6 copy-done
  8.1 2.7 convolution_multiply_fusion
  10.8 159.4 %reduce-scatter.2.cloned.1.call-done = f32[16,16,256]{2,1,0:T(8,128)} async-done(((f32[16,256,256]{2,1,0:T(8,128)}), f32[16,16,256]{2,1,0:T(8,128)}) %reduce-scatter.2.cloned.1.call-update) | async-done | bytes 262160 | tf_op jit(solution)/shard_map/reduce_scatter | solution.py:47
  170.2 5.9 %all-to-all-start = ((f32[16,16,256]{2,1,0:T(8,128)}), f32[16,16,256]{2,1,0:T(8,128)S(1)}, u32[]{:S(2)}, u32[]{:S(2)}) async-start(f32[16,16,256]{2,1,0:T(8,128)} %reduce-scatter.2.cloned.1.call-done), calls=%async_computation.1 | async-start | bytes 524288 | tf_op jit(solution)/shard_map/all_to_all | solution.py:60
  176.6 1.2 select_reduce_fusion
  178.0 8.8 %psum.35 = f32[32]{0:T(128)S(1)} all-reduce(f32[32]{0:T(128)S(1)} %convolution_bitcast_fusion.2), channel_id=1, replica_groups=mesh['dp_0'=4,'dp_1'=2,'dp_2'=2,'mp_0'=8,'mp_1'=4] {'dp_0'}, use_global_device_ids=true, to_apply=%region_2.3 | all-reduce | flops 32 | bytes 256 | tf_op jit(solution)/shard_map/psum | solution.py:15
  186.8 12.5 %psum.36 = f32[32]{0:T(128)S(1)} all-reduce(f32[32]{0:T(128)S(1)} %psum.35), channel_id=1, replica_groups=mesh['dp_0'=4,'dp_1'=2,'dp_2'=2,'mp_0'=8,'mp_1'=4] {'dp_1'}, use_global_device_ids=true, to_apply=%region_3.4 | all-reduce | flops 32 | bytes 256 | tf_op jit(solution)/shard_map/psum | solution.py:15
  199.3 5.4 %psum.37 = f32[32]{0:T(128)S(1)} all-reduce(f32[32]{0:T(128)S(1)} %psum.36), channel_id=1, replica_groups=mesh['dp_0'=4,'dp_1'=2,'dp_2'=2,'mp_0'=8,'mp_1'=4] {'dp_2'}, use_global_device_ids=true, to_apply=%region_4.5 | all-reduce | flops 32 | bytes 256 | tf_op jit(solution)/shard_map/psum | solution.py:15
  204.7 28.7 %psum.38 = f32[32]{0:T(128)S(1)} all-reduce(f32[32]{0:T(128)S(1)} %psum.37), channel_id=1, replica_groups=mesh['dp_0'=4,'dp_1'=2,'dp_2'=2,'mp_0'=8,'mp_1'=4] {'mp_0'}, use_global_device_ids=true, to_apply=%region_5.6 | all-reduce | flops 32 | bytes 256 | tf_op jit(solution)/shard_map/psum | solution.py:15
  233.4 8.4 %psum.39 = f32[32]{0:T(128)S(1)} all-reduce(f32[32]{0:T(128)S(1)} %psum.38), channel_id=1, replica_groups=mesh['dp_0'=4,'dp_1'=2,'dp_2'=2,'mp_0'=8,'mp_1'=4] {'mp_1'}, use_global_device_ids=true, to_apply=%region_6.7 | all-reduce | flops 32 | bytes 256 | tf_op jit(solution)/shard_map/psum | solution.py:15
  241.9 0.6 dynamic_slice.11
  242.5 1.4 multiply_reduce_fusion
  244.7 0.8 multiply_subtract_fusion
  247.1 0.7 fusion.5
  249.8 0.4 fusion.10
  251.0 0.4 fusion.11
  251.4 0.4 fusion.12
  252.6 0.4 fusion.13
  253.0 0.4 fusion.14
  254.6 0.4 fusion.16
  255.7 0.4 fusion.17
  256.2 0.4 fusion.18
  258.0 33.6 %all_to_all.21 = f32[1,256,256]{2,0,1:T(1,128)S(1)} all-to-all(f32[1,256,256]{2,0,1:T(1,128)S(1)} %copy.8), channel_id=1, replica_groups=mesh['dp_0'=4,'dp_1'=2,'dp_2'=2,'mp_0'=8,'mp_1'=4] {'dp_0','dp_1','dp_2'}, dimensions={1} | all-to-all | bytes 524288 | tf_op jit(solution)/shard_map/all_to_all | solution.py:67
  291.6 0.7 copy.9
  (35 shorter events, 9.1 us)
Async XLA Ops:
  6.5 1.6 copy-start
  6.5 169.6 %copy-start.1 = (s32[512]{0:T(512)S(1)}, s32[512]{0:T(512)}, u32[]{:S(2)}) copy-start(s32[512]{0:T(512)} %param.3) | copy-start | bytes 6148
  6.5 163.7 %reduce-scatter.2.cloned.1.call-start = ((), (), s32[]{:S(2)}) async-start(), calls=%async_computation.3 | async-start | bytes 4456448 | tf_op jit(solution)/shard_map/reduce_scatter | solution.py:47
  170.2 72.3 %all-to-all-start = ((f32[16,16,256]{2,1,0:T(8,128)}), f32[16,16,256]{2,1,0:T(8,128)S(1)}, u32[]{:S(2)}, u32[]{:S(2)}) async-start(f32[16,16,256]{2,1,0:T(8,128)} %reduce-scatter.2.cloned.1.call-done), calls=%async_computation.1 | async-start | bytes 524288 | tf_op jit(solution)/shard_map/all_to_all | solution.py:60
Sparse Core Ops, SparseCore 0:
  12.3 157.9 reduce-scatter.1
where the time goes:
time: 300 us; the launch traced here: 299 us
  waiting for transfers between devices  159 us (53%)
  blocking collectives  97.4 us (32%)
  between operations  14.4 us (5%)
  matrix products  14.3 us (5%)
  starting transfers between devices  5.94 us (2%)
  other arithmetic  4.21 us (1%)
  local copies, waits for them, and re-layouts  3.44 us (1%)
    reduce_scatter x1, waiting for transfers between devices, local(): mine = lax.psum_scatter(partial_value, DP, scatter_dimension=1, tiled=True)  159 us
    psum x5, blocking collectives, over_axes(): array = lax.psum(array, axis)  63.8 us
    all_to_all x1, blocking collectives, local(): lax.all_to_all(solved, DP, split_axis=1, concat_axis=0, tiled=True)  33.6 us
  transfers between devices with their start and end apart: 2, of which 1 were waited for; matrix products, arithmetic and copies ran while one was open for 1% of the time, Pallas kernels for 0%

commit v1 on v0

v1 whole, which is shorter than its diff:
```python
import jax
import jax.numpy as jnp
from jax import lax
from jax.experimental import pallas as pl
from jax.experimental.pallas import tpu as pltpu
from jax.sharding import Mesh
from jax.sharding import PartitionSpec as P


ITERS = 8
FULL_STEPS = 1
ORDER = 256
HALF = 128
ROWS = 264
DP = ("y", "zh", "c")
MP = ("zl", "x")


def _iotas(shape):
    return lax.broadcasted_iota(jnp.int32, shape, 0), lax.broadcasted_iota(jnp.int32, shape, 1)


def _nt(a, b):
    return lax.dot_general(a, b, (((1,), (1,)), ((), ())), preferred_element_type=jnp.float32)


def _stats_kernel(where_ref, layers_ref, grad_ref, send_ref, own_ref):
    core, holder = where_ref[0], where_ref[1]
    holders = 32
    blocks = grad_ref.shape[0]
    half = blocks // 2
    row, col = _iotas((HALF, HALF))
    lane = lax.broadcasted_iota(jnp.int32, (1, HALF), 1)
    sums = jnp.zeros((1, HALF), jnp.float32)
    diagonals = []
    for out_ref, first in ((send_ref, (1 - core) * half), (own_ref, core * half)):
        for k in range(half):
            gradient = grad_ref[first + k]
            top = _nt(gradient[:HALF], gradient)
            low = _nt(gradient[HALF:], gradient[HALF:])
            left = top[:, :HALF]
            out_ref[k, 0:HALF, :] = top[:, HALF:]
            out_ref[k, HALF : 2 * HALF, :] = jnp.where(row > col, left, low)
            on = row == col
            diag_left = jnp.sum(jnp.where(on, left, 0.0), axis=0, keepdims=True)
            diag_low = jnp.sum(jnp.where(on, low, 0.0), axis=0, keepdims=True)
            diagonals.append((out_ref, k, diag_left))
            trace = jnp.sum(diag_left + diag_low, axis=1, keepdims=True)
            layer = layers_ref[(first + k) * holders + holder]
            sums = sums + jnp.where(lane == layer, trace, 0.0)
    tail_row, _ = _iotas((8, HALF))
    for out_ref, k, diag_left in diagonals:
        out_ref[k, 2 * HALF :, :] = jnp.where(tail_row == 0, diag_left, jnp.where(tail_row == 1, sums, 0.0))


def _split(a):
    high = a.astype(jnp.bfloat16)
    return high, (a - high.astype(jnp.float32)).astype(jnp.bfloat16)


def _dot(a, b):
    return jnp.dot(a, b, preferred_element_type=jnp.float32)


def _product(a, b):
    return _dot(a[0], b[0]) + (_dot(a[0], b[1]) + _dot(a[1], b[0]))


def _full(a, b):
    return jnp.dot(a, b, precision=lax.Precision.HIGHEST, preferred_element_type=jnp.float32)


def _unpack(packed):
    row, col = _iotas((HALF, HALF))
    corner = packed[0:HALF]
    both = packed[HALF : 2 * HALF]
    flipped = both.T
    left = jnp.where(row > col, both, jnp.where(row < col, flipped, packed[2 * HALF : 2 * HALF + 1]))
    low = jnp.where(row <= col, both, flipped)
    return jnp.concatenate([jnp.concatenate([left, corner], 1), jnp.concatenate([corner.T, low], 1)], 0)


def _solve_kernel(where_ref, layers_ref, map_ref, own_ref, other_ref, sums_ref, out_ref, first_ref):
    core, line, side, holder = where_ref[0], where_ref[1], where_ref[2], where_ref[3]
    count = own_ref.shape[0]
    row, col = _iotas((ORDER, ORDER))
    on = row == col
    lane = lax.broadcasted_iota(jnp.int32, (1, HALF), 1)
    totals = jnp.sum(sums_ref[...], axis=0, keepdims=True) * (1.0 / 4096.0)
    coupled, factor, current = [], [], []
    for k in range(count):
        stats = _unpack((own_ref[k] + other_ref[k]) * (1.0 / 4096.0))
        layer = layers_ref[((core * 4 + line) * count + k) * 32 + holder]
        members = jnp.sum(jnp.where(map_ref[...] == layer, 1.0, 0.0), axis=(0, 1), keepdims=True)
        total = jnp.sum(jnp.where(lane == layer, totals, 0.0), axis=1, keepdims=True)
        ridge = 0.1 * total / (members * ORDER)
        damped = stats + jnp.where(on, ridge, 0.0)
        squares = jnp.sum(damped * damped, axis=(0, 1), keepdims=True)
        scaled = 2.5 / jnp.sqrt(squares)
        root = jnp.sqrt(jnp.sqrt(scaled))
        coupled.append(scaled * damped)
        factor.append(jnp.where(on, 1.25, 0.0) - 0.25 * coupled[k])
        first_ref[k] = root * factor[k]
        current.append(jnp.concatenate([first_ref[k, pl.ds(q * 64 + side * 32, 32), :] for q in range(4)], 0))
    for step in range(ITERS - 1):
        for k in range(count):
            if step < FULL_STEPS:
                square = _full(factor[k], factor[k])
                fourth = _full(square, square)
                coupled[k] = _full(fourth, coupled[k])
            else:
                parts = _split(factor[k])
                square = _split(_product(parts, parts))
                fourth = _split(_product(square, square))
                coupled[k] = _product(fourth, _split(coupled[k]))
            factor[k] = jnp.where(on, 1.25, 0.0) - 0.25 * coupled[k]
        for k in range(count):
            current[k] = _product(_split(current[k]), _split(factor[k]))
    for k in range(count):
        for c in range(2):
            for q in range(4):
                out_ref[c * 4 + q, k] = current[k][(q * 2 + c) * 16 : (q * 2 + c) * 16 + 16]


def _smem():
    return pl.BlockSpec(memory_space=pltpu.SMEM)


def _vmem():
    return pl.BlockSpec(memory_space=pltpu.VMEM)


def local(grads, layer_map):
    gradient = grads[0, :, 0]
    core, line, side = lax.axis_index("c"), lax.axis_index("y"), lax.axis_index("zh")
    holder = lax.axis_index(MP)
    half = gradient.shape[0] // 2
    pack = jax.ShapeDtypeStruct((half, ROWS, HALF), jnp.float32)
    send, own = pl.pallas_call(
        _stats_kernel,
        out_shape=(pack, pack),
        in_specs=[_smem(), _smem(), _vmem()],
        out_specs=(_vmem(), _vmem()),
        compiler_params=pltpu.CompilerParams(vmem_limit_bytes=16 * 2**20),
        name="stats",
    )(jnp.stack([core, holder]).astype(jnp.int32), layer_map, gradient)
    got = lax.ppermute(send, "c", [(0, 1), (1, 0)])
    chip = own + got
    pieces = lax.all_to_all(chip, "y", 0, 0, tiled=True)
    mine = jnp.sum(pieces.reshape(4, half // 4, ROWS, HALF), axis=0)
    other = lax.ppermute(mine, "zh", [(0, 1), (1, 0)])
    row = jnp.broadcast_to(mine[0, 2 * HALF + 1][None, None], (64, 1, HALF))
    sums = lax.all_to_all(row, ("zh", "zl", "x"), 0, 0, tiled=True)
    rows = pl.pallas_call(
        _solve_kernel,
        out_shape=jax.ShapeDtypeStruct((8, half // 4, 16, ORDER), jnp.float32),
        in_specs=[_smem(), _smem(), _vmem(), _vmem(), _vmem(), _vmem()],
        out_specs=_vmem(),
        scratch_shapes=[pltpu.VMEM((half // 4, ORDER, ORDER), jnp.float32)],
        compiler_params=pltpu.CompilerParams(vmem_limit_bytes=16 * 2**20),
        name="solve",
    )(
        jnp.stack([core, line, side, holder]).astype(jnp.int32),
        layer_map,
        layer_map.reshape(4, HALF),
        mine,
        other,
        sums.reshape(64, HALF),
    )
    back = lax.all_to_all(rows, ("c", "y"), 0, 0, tiled=True)
    return back.reshape(16, 1, 16, ORDER)


def solution(mesh):
    torus = Mesh(mesh.devices.reshape(4, 2, 2, 8, 4), ("y", "zh", "c", "zl", "x"))
    in_specs = (P(DP, None, MP, None, None), P())
    out_specs = P(None, MP, DP, None)
    return jax.shard_map(local, mesh=torus, in_specs=in_specs, out_specs=out_specs, check_vma=False)
```

time: 300 us -> 100 us (0.33)
  waiting for transfers between devices: 159 us -> 25.2 us
  blocking collectives: 97.4 us -> 29.1 us
  starting transfers between devices: 5.94 us -> 28.4 us
  between operations: 14.4 us -> 0.06 us
  matrix products: 14.3 us -> 0 us
  Pallas kernels: 0 us -> 12.8 us
  other arithmetic: 4.21 us -> 0.34 us
    reduce_scatter x1 -> x0, waiting for transfers between devices: 159 us -> none  [local(): mine = lax.psum_scatter(partial_value, DP, scatter_dimension=1, tiled=True)]
    psum x5 -> x0, blocking collectives: 63.8 us -> none  [over_axes(): array = lax.psum(array, axis)]
    all_to_all x1, waiting for transfers between devices: 0.01 us -> 22.9 us  [local(): sums = lax.all_to_all(row, ('zh', 'zl', 'x'), 0, 0, tiled=True)]
    ppermute x0 -> x2, starting transfers between devices: none -> 20.2 us  [the longest x1 11.5 us: local(): other = lax.ppermute(mine, 'zh', [(0, 1), (1, 0)])]
    dot_general x32 -> x0, matrix products: 14.3 us -> none  [the longest x8 3.21 us: newton_root(): jnp.einsum('sij,sjk->sik', current, factor, precision=lax.Precision.HIGHEST)]
    pallas_call x0 -> x2, Pallas kernels: none -> 12.8 us  [the longest x1 11.2 us: local(): pl.pallas_call(_solve_kernel, out_shape=jax.ShapeDtypeStruct((8, half //...]
    all_to_all x1 -> x2, blocking collectives: 33.6 us -> 29.1 us  [the longest x1 17.5 us: local(): pieces = lax.all_to_all(chip, 'y', 0, 0, tiled=True)]
  transfers between devices with their start and end apart: 2 -> 3, of which waited for: 1 -> 2; matrix products, arithmetic and copies ran while one was open for 1% -> 1% of each run, Pallas kernels for 0% -> 0%
where the time goes in v1:
time: 100 us; the launch traced here: 99.6 us
  blocking collectives  29.1 us (29%)
  starting transfers between devices  28.4 us (28%)
  waiting for transfers between devices  25.2 us (25%)
  Pallas kernels  12.8 us (13%)
  local copies, waits for them, and re-layouts  3.61 us (4%)
    all_to_all x1, waiting for transfers between devices, local(): sums = lax.all_to_all(row, ('zh', 'zl', 'x'), 0, 0, tiled=True)  22.9 us
    all_to_all x1, blocking collectives, local(): pieces = lax.all_to_all(chip, 'y', 0, 0, tiled=True)  17.5 us
    all_to_all x1, blocking collectives, local(): back = lax.all_to_all(rows, ('c', 'y'), 0, 0, tiled=True)  11.6 us
    ppermute x1, starting transfers between devices, local(): other = lax.ppermute(mine, 'zh', [(0, 1), (1, 0)])  11.5 us
    pallas_call x1, Pallas kernels, local(): pl.pallas_call(_solve_kernel, out_shape=jax.ShapeDtypeStruct((8, half //...  11.2 us
    ppermute x1, starting transfers between devices, local(): got = lax.ppermute(send, 'c', [(0, 1), (1, 0)])  8.74 us
    all_to_all x1, starting transfers between devices, local(): sums = lax.all_to_all(row, ('zh', 'zl', 'x'), 0, 0, tiled=True)  8.21 us
    unnamed x7, local copies, waits for them, and re-layouts  2.98 us
  transfers between devices with their start and end apart: 3, of which 2 were waited for; matrix products, arithmetic and copies ran while one was open for 1% of the time, Pallas kernels for 0%

profile of v1, /device:TPU:1, one launch (start us, length us, event | category | flops | bytes accessed | tf_op | source)
XLA Modules:
  0.0 99.6 jit_solution(14863491773944277663)
XLA Ops:
  0.0 0.1 pad_add_fusion.1.where_ref
  0.1 0.0 copy-start
  0.1 1.6 %copy-done = bf16[1,16,1,256,256]{4,3,2,1,0:T(8,128)(2,1)S(1)} copy-done((bf16[1,16,1,256,256]{4,3,2,1,0:T(8,128)(2,1)S(1)}, bf16[1,16,1,256,256]{4,3,2,1,0:T(8,128)(2,1)}, u32[]{:S(2)}) %copy-start) | copy-done | bytes 2097176
  1.7 0.0 copy-start.1
  1.7 0.7 copy-done.1
  2.3 1.7 %stats.1 = (f32[8,264,128]{2,1,0:T(8,128)S(1)}, f32[8,264,128]{2,1,0:T(8,128)S(1)}) custom-call(s32[2]{0:T(128)S(1)} %pad_add_fusion.1.where_ref, s32[512]{0:T(512)S(1)} %copy-done.1, bf16[16,256,256]{2,1,0:T(8,128)(2,1)S(1)} %bitcast.13), custom_call_target="tpu_custom_call" | custom-call | tf_op jit(solution)/shard_map/stats/pallas_call | solution.py:139
  4.0 8.7 %collective-permute-start = (f32[8,264,128]{2,1,0:T(8,128)S(1)}, f32[8,264,128]{2,1,0:T(8,128)S(1)}, u32[]{:S(2)}, u32[]{:S(2)}) collective-permute-start(f32[8,264,128]{2,1,0:T(8,128)S(1)} %get-tuple-element.8), channel_id=1, source_target_pairs={{0,32},{32,0},{1,33},{33,1},{2,34},{34,2},{3,35},{35,3},{4,36},{36... | collective-permute-start | bytes 3244040 | tf_op jit(solution)/shard_map/ppermute | solution.py:147
  12.8 2.3 %collective-permute-done = f32[8,264,128]{2,1,0:T(8,128)S(1)} collective-permute-done((f32[8,264,128]{2,1,0:T(8,128)S(1)}, f32[8,264,128]{2,1,0:T(8,128)S(1)}, u32[]{:S(2)}, u32[]{:S(2)}) %collective-permute-start) | collective-permute-done | bytes 1081376 | tf_op jit(solution)/shard_map/ppermute | solution.py:147
  15.1 0.1 add.7
  15.2 17.5 %all_to_all.15 = f32[8,264,128]{2,1,0:T(8,128)S(1)} all-to-all(f32[8,264,128]{2,1,0:T(8,128)S(1)} %add.7), channel_id=1, replica_groups=mesh['y'=4,'zh'=2,'c'=2,'zl'=8,'x'=4] {'y'}, dimensions={0} | all-to-all | bytes 2162688 | tf_op jit(solution)/shard_map/all_to_all | solution.py:149
  32.7 0.0 copy-start.2
  32.7 0.1 reduce_sum.9.own_ref
  32.7 11.5 %collective-permute-start.1 = (f32[2,264,128]{2,1,0:T(8,128)S(1)}, f32[2,264,128]{2,1,0:T(8,128)S(1)}, u32[]{:S(2)}, u32[]{:S(2)}) collective-permute-start(f32[2,264,128]{2,1,0:T(8,128)S(1)} %reduce_sum.9.own_ref), channel_id=1, source_target_pairs={{0,64},{64,0},{1,65},{65,1},{2,66},{66,2},{3,67},{67,3},{4,68},{68... | collective-permute-start | bytes 811016 | tf_op jit(solution)/shard_map/ppermute | solution.py:151
  44.3 0.6 broadcast_in_dim.8
  44.9 8.2 %all-to-all-start.1 = ((f32[64,1,128]{2,1,0:T(1,128)}), f32[64,1,128]{2,1,0:T(1,128)S(1)}, u32[]{:S(2)}, u32[]{:S(2)}) async-start(f32[64,1,128]{2,1,0:T(1,128)} %broadcast_in_dim.8), calls=%async_computation.1 | async-start | bytes 65536 | tf_op jit(solution)/shard_map/all_to_all | solution.py:153
  53.1 0.1 pad_add_fusion.where_ref
  53.2 22.9 %all-to-all-done.1 = f32[64,1,128]{2,1,0:T(1,128)S(1)} async-done(((f32[64,1,128]{2,1,0:T(1,128)}), f32[64,1,128]{2,1,0:T(1,128)S(1)}, u32[]{:S(2)}, u32[]{:S(2)}) %all-to-all-start.1) | async-done | bytes 32800 | tf_op jit(solution)/shard_map/all_to_all | solution.py:153
  76.1 0.0 collective-permute-done.1.other_ref
  76.1 0.0 copy-done.2
  76.1 11.2 %solve.1 = f32[8,2,16,256]{3,2,1,0:T(8,128)S(1)} custom-call(s32[4]{0:T(128)S(1)} %pad_add_fusion.where_ref, s32[512]{0:T(512)S(1)} %copy-done.2, s32[4,128]{1,0:T(4,128)S(1)} %bitcast.15, f32[2,264,128]{2,1,0:T(8,128)S(1)} %reduce_sum.9.own_ref, f32[2,264,128]{2,1,0:T(8,128)S(1)} %collective-permute-done.1.other_ref, f32[64,128]{1,0:T(8,128)S(1)} %bitcast.14), custom_call_target="tpu_custom_call" | custom-call | tf_op jit(solution)/shard_map/solve/pallas_call | solution.py:154
  87.3 11.6 %all_to_all.16 = f32[8,2,16,256]{3,2,1,0:T(8,128)S(1)} all-to-all(f32[8,2,16,256]{3,2,1,0:T(8,128)S(1)} %solve.1), channel_id=1, replica_groups=mesh['y'=4,'zh'=2,'c'=2,'zl'=8,'x'=4] {'c','y'}, dimensions={0} | all-to-all | bytes 524288 | tf_op jit(solution)/shard_map/all_to_all | solution.py:170
  98.9 0.7 copy.6
  (1 shorter events, 0.0 us)
Async XLA Ops:
  0.1 1.6 %copy-start = (bf16[1,16,1,256,256]{4,3,2,1,0:T(8,128)(2,1)S(1)}, bf16[1,16,1,256,256]{4,3,2,1,0:T(8,128)(2,1)}, u32[]{:S(2)}) copy-start(bf16[1,16,1,256,256]{4,3,2,1,0:T(8,128)(2,1)} %param.2) | copy-start | bytes 6291460
  1.7 0.7 copy-start.1
  4.0 11.1 %collective-permute-start = (f32[8,264,128]{2,1,0:T(8,128)S(1)}, f32[8,264,128]{2,1,0:T(8,128)S(1)}, u32[]{:S(2)}, u32[]{:S(2)}) collective-permute-start(f32[8,264,128]{2,1,0:T(8,128)S(1)} %get-tuple-element.8), channel_id=1, source_target_pairs={{0,32},{32,0},{1,33},{33,1},{2,34},{34,2},{3,35},{35,3},{4,36},{36... | collective-permute-start | bytes 3244040 | tf_op jit(solution)/shard_map/ppermute | solution.py:147
  32.7 43.5 %copy-start.2 = (s32[512]{0:T(512)S(1)}, s32[512]{0:T(512)}, u32[]{:S(2)}) copy-start(s32[512]{0:T(512)} %layers_ref.3) | copy-start | bytes 6148
  32.7 43.4 %collective-permute-start.1 = (f32[2,264,128]{2,1,0:T(8,128)S(1)}, f32[2,264,128]{2,1,0:T(8,128)S(1)}, u32[]{:S(2)}, u32[]{:S(2)}) collective-permute-start(f32[2,264,128]{2,1,0:T(8,128)S(1)} %reduce_sum.9.own_ref), channel_id=1, source_target_pairs={{0,64},{64,0},{1,65},{65,1},{2,66},{66,2},{3,67},{67,3},{4,68},{68... | collective-permute-start | bytes 811016 | tf_op jit(solution)/shard_map/ppermute | solution.py:151
  44.9 31.2 %all-to-all-start.1 = ((f32[64,1,128]{2,1,0:T(1,128)}), f32[64,1,128]{2,1,0:T(1,128)S(1)}, u32[]{:S(2)}, u32[]{:S(2)}) async-start(f32[64,1,128]{2,1,0:T(1,128)} %broadcast_in_dim.8), calls=%async_computation.1 | async-start | bytes 65536 | tf_op jit(solution)/shard_map/all_to_all | solution.py:153

commit v2 on v1

--- a/solution.py
+++ b/solution.py
@@ -81,45 +81,36 @@
 
 
 def _solve_kernel(where_ref, layers_ref, map_ref, own_ref, other_ref, sums_ref, out_ref, first_ref):
-    core, line, side, holder = where_ref[0], where_ref[1], where_ref[2], where_ref[3]
-    count = own_ref.shape[0]
+    side, block = where_ref[0], where_ref[1]
     row, col = _iotas((ORDER, ORDER))
     on = row == col
     lane = lax.broadcasted_iota(jnp.int32, (1, HALF), 1)
+    stats = _unpack((own_ref[...] + other_ref[...]) * (1.0 / 4096.0))
+    layer = layers_ref[block]
+    members = jnp.sum(jnp.where(map_ref[...] == layer, 1.0, 0.0), axis=(0, 1), keepdims=True)
     totals = jnp.sum(sums_ref[...], axis=0, keepdims=True) * (1.0 / 4096.0)
-    coupled, factor, current = [], [], []
-    for k in range(count):
-        stats = _unpack((own_ref[k] + other_ref[k]) * (1.0 / 4096.0))
-        layer = layers_ref[((core * 4 + line) * count + k) * 32 + holder]
-        members = jnp.sum(jnp.where(map_ref[...] == layer, 1.0, 0.0), axis=(0, 1), keepdims=True)
-        total = jnp.sum(jnp.where(lane == layer, totals, 0.0), axis=1, keepdims=True)
-        ridge = 0.1 * total / (members * ORDER)
-        damped = stats + jnp.where(on, ridge, 0.0)
-        squares = jnp.sum(damped * damped, axis=(0, 1), keepdims=True)
-        scaled = 2.5 / jnp.sqrt(squares)
-        root = jnp.sqrt(jnp.sqrt(scaled))
-        coupled.append(scaled * damped)
-        factor.append(jnp.where(on, 1.25, 0.0) - 0.25 * coupled[k])
-        first_ref[k] = root * factor[k]
-        current.append(jnp.concatenate([first_ref[k, pl.ds(q * 64 + side * 32, 32), :] for q in range(4)], 0))
+    total = jnp.sum(jnp.where(lane == layer, totals, 0.0), axis=1, keepdims=True)
+    damped = stats + jnp.where(on, 0.1 * total / (members * ORDER), 0.0)
+    scaled = 2.5 / jnp.sqrt(jnp.sum(damped * damped, axis=(0, 1), keepdims=True))
+    coupled = scaled * damped
+    factor = jnp.where(on, 1.25, 0.0) - 0.25 * coupled
+    first_ref[...] = jnp.sqrt(jnp.sqrt(scaled)) * factor
+    current = jnp.concatenate([first_ref[pl.ds(q * 64 + side * 32, 32), :] for q in range(4)], 0)
     for step in range(ITERS - 1):
-        for k in range(count):
-            if step < FULL_STEPS:
-                square = _full(factor[k], factor[k])
-                fourth = _full(square, square)
-                coupled[k] = _full(fourth, coupled[k])
-            else:
-                parts = _split(factor[k])
-                square = _split(_product(parts, parts))
-                fourth = _split(_product(square, square))
-                coupled[k] = _product(fourth, _split(coupled[k]))
-            factor[k] = jnp.where(on, 1.25, 0.0) - 0.25 * coupled[k]
-        for k in range(count):
-            current[k] = _product(_split(current[k]), _split(factor[k]))
-    for k in range(count):
-        for c in range(2):
-            for q in range(4):
-                out_ref[c * 4 + q, k] = current[k][(q * 2 + c) * 16 : (q * 2 + c) * 16 + 16]
+        if step < FULL_STEPS:
+            square = _full(factor, factor)
+            fourth = _full(square, square)
+            coupled = _full(fourth, coupled)
+        else:
+            parts = _split(factor)
+            square = _split(_product(parts, parts))
+            fourth = _split(_product(square, square))
+            coupled = _product(fourth, _split(coupled))
+        factor = jnp.where(on, 1.25, 0.0) - 0.25 * coupled
+        current = _product(_split(current), _split(factor))
+    for c in range(2):
+        for q in range(4):
+            out_ref[c * 4 + q] = current[(q * 2 + c) * 16 : (q * 2 + c) * 16 + 16]
 
 
 def _smem():
@@ -145,30 +136,28 @@
         name="stats",
     )(jnp.stack([core, holder]).astype(jnp.int32), layer_map, gradient)
     got = lax.ppermute(send, "c", [(0, 1), (1, 0)])
-    chip = own + got
-    pieces = lax.all_to_all(chip, "y", 0, 0, tiled=True)
-    mine = jnp.sum(pieces.reshape(4, half // 4, ROWS, HALF), axis=0)
-    other = lax.ppermute(mine, "zh", [(0, 1), (1, 0)])
-    row = jnp.broadcast_to(mine[0, 2 * HALF + 1][None, None], (64, 1, HALF))
-    sums = lax.all_to_all(row, ("zh", "zl", "x"), 0, 0, tiled=True)
-    rows = pl.pallas_call(
-        _solve_kernel,
-        out_shape=jax.ShapeDtypeStruct((8, half // 4, 16, ORDER), jnp.float32),
-        in_specs=[_smem(), _smem(), _vmem(), _vmem(), _vmem(), _vmem()],
-        out_specs=_vmem(),
-        scratch_shapes=[pltpu.VMEM((half // 4, ORDER, ORDER), jnp.float32)],
-        compiler_params=pltpu.CompilerParams(vmem_limit_bytes=16 * 2**20),
-        name="solve",
-    )(
-        jnp.stack([core, line, side, holder]).astype(jnp.int32),
-        layer_map,
-        layer_map.reshape(4, HALF),
-        mine,
-        other,
-        sums.reshape(64, HALF),
-    )
-    back = lax.all_to_all(rows, ("c", "y"), 0, 0, tiled=True)
-    return back.reshape(16, 1, 16, ORDER)
+    chip = [own[4 * k : 4 * k + 4] + got[4 * k : 4 * k + 4] for k in range(half // 4)]
+    mine, other = [], []
+    for k in range(half // 4):
+        pieces = lax.all_to_all(chip[k], "y", 0, 0, tiled=True)
+        mine.append(jnp.sum(pieces, axis=0))
+        other.append(lax.ppermute(mine[k], "zh", [(0, 1), (1, 0)]))
+    row = jnp.broadcast_to(mine[0][2 * HALF + 1][None, None], (64, 1, HALF))
+    sums = lax.all_to_all(row, ("zh", "zl", "x"), 0, 0, tiled=True).reshape(64, HALF)
+    back = []
+    for k in range(half // 4):
+        block = ((core * (half // 4) + k) * 4 + line) * 32 + holder
+        rows = pl.pallas_call(
+            _solve_kernel,
+            out_shape=jax.ShapeDtypeStruct((8, 16, ORDER), jnp.float32),
+            in_specs=[_smem(), _smem()] + [_vmem()] * 4,
+            out_specs=_vmem(),
+            scratch_shapes=[pltpu.VMEM((ORDER, ORDER), jnp.float32)],
+            compiler_params=pltpu.CompilerParams(vmem_limit_bytes=16 * 2**20),
+            name="solve",
+        )(jnp.stack([side, block]).astype(jnp.int32), layer_map, layer_map.reshape(4, HALF), mine[k], other[k], sums)
+        back.append(lax.all_to_all(rows, ("c", "y"), 0, 0, tiled=True).reshape(2, 4, 16, ORDER))
+    return jnp.stack(back, axis=1).reshape(16, 1, 16, ORDER)
 
 
 def solution(mesh):

time: 100 us -> 104 us (1.040)
  starting transfers between devices: 28.4 us -> 53.9 us
  waiting for transfers between devices: 25.2 us -> 3.9 us
  blocking collectives: 29.1 us -> 21.5 us
  Pallas kernels: 12.8 us -> 19.6 us
    all_to_all x1 -> x3, waiting for transfers between devices: 22.9 us -> 1.58 us  [the longest x1 1.57 us: local(): lax.all_to_all(row, ('zh', 'zl', 'x'), 0, 0, tiled=True).reshape(64, HALF)]
    all_to_all x1 -> x3, starting transfers between devices: 8.21 us -> 22 us  [the longest x1 10.7 us: local(): lax.all_to_all(row, ('zh', 'zl', 'x'), 0, 0, tiled=True).reshape(64, HALF)]
    ppermute x1 -> x2, starting transfers between devices: 11.5 us -> 23.2 us  [local(): other.append(lax.ppermute(mine[k], 'zh', [(0, 1), (1, 0)]))]
    all_to_all x2, blocking collectives: 29.1 us -> 21.5 us  [the longest x1 11.7 us: local(): pieces = lax.all_to_all(chip[k], 'y', 0, 0, tiled=True)]
    pallas_call x1 -> x2, Pallas kernels: 11.2 us -> 17.9 us  [local(): pl.pallas_call(_solve_kernel, out_shape=jax.ShapeDtypeStruct((8, 16, ORDE...]
    unnamed x7 -> x6, local copies, waits for them, and re-layouts: 2.98 us -> 2.28 us
  transfers between devices with their start and end apart: 3 -> 6, of which waited for: 2 -> 2; matrix products, arithmetic and copies ran while one was open for 1% -> 1% of each run, Pallas kernels for 0% -> 17%
where the time goes in v2:
time: 104 us
  starting transfers between devices  53.9 us (52%)
  blocking collectives  21.5 us (21%)
  Pallas kernels  19.6 us (19%)
  waiting for transfers between devices  3.9 us (4%)
  local copies, waits for them, and re-layouts  3.63 us (3%)
  other arithmetic  1.21 us (1%)
    ppermute x2, starting transfers between devices, local(): other.append(lax.ppermute(mine[k], 'zh', [(0, 1), (1, 0)]))  23.2 us
    pallas_call x2, Pallas kernels, local(): pl.pallas_call(_solve_kernel, out_shape=jax.ShapeDtypeStruct((8, 16, ORDE...  17.9 us
    all_to_all x1, blocking collectives, local(): pieces = lax.all_to_all(chip[k], 'y', 0, 0, tiled=True)  11.7 us
    all_to_all x1, starting transfers between devices, local(): lax.all_to_all(row, ('zh', 'zl', 'x'), 0, 0, tiled=True).reshape(64, HALF)  10.7 us
    all_to_all x1, blocking collectives, local(): lax.all_to_all(rows, ('c', 'y'), 0, 0, tiled=True).reshape(2, 4, 16, ORDER)  9.77 us
    ppermute x1, starting transfers between devices, local(): got = lax.ppermute(send, 'c', [(0, 1), (1, 0)])  8.74 us
    all_to_all x1, starting transfers between devices, local(): lax.all_to_all(rows, ('c', 'y'), 0, 0, tiled=True).reshape(2, 4, 16, ORDER)  7.74 us
    all_to_all x1, starting transfers between devices, local(): pieces = lax.all_to_all(chip[k], 'y', 0, 0, tiled=True)  3.6 us
  transfers between devices with their start and end apart: 6, of which 2 were waited for; matrix products, arithmetic and copies ran while one was open for 1% of the time, Pallas kernels for 17%

profile of v2, /device:TPU:1, one launch (start us, length us, event | category | flops | bytes accessed | tf_op | source)
XLA Modules:
  0.0 103.9 jit_solution(3748648388924030904)
XLA Ops:
  0.0 0.1 pad_add_fusion.1.where_ref
  0.1 1.6 %copy-done = bf16[1,16,1,256,256]{4,3,2,1,0:T(8,128)(2,1)S(1)} copy-done((bf16[1,16,1,256,256]{4,3,2,1,0:T(8,128)(2,1)S(1)}, bf16[1,16,1,256,256]{4,3,2,1,0:T(8,128)(2,1)}, u32[]{:S(2)}) %copy-start) | copy-done | bytes 2097176
  1.7 0.7 copy-done.1
  2.3 1.7 %stats.1 = (f32[8,264,128]{2,1,0:T(8,128)S(1)}, f32[8,264,128]{2,1,0:T(8,128)S(1)}) custom-call(s32[2]{0:T(128)S(1)} %pad_add_fusion.1.where_ref, s32[512]{0:T(512)S(1)} %copy-done.1, bf16[16,256,256]{2,1,0:T(8,128)(2,1)S(1)} %bitcast.13), custom_call_target="tpu_custom_call" | custom-call | tf_op jit(solution)/shard_map/stats/pallas_call | solution.py:130
  4.0 8.7 %collective-permute-start = (f32[8,264,128]{2,1,0:T(8,128)S(1)}, f32[8,264,128]{2,1,0:T(8,128)S(1)}, u32[]{:S(2)}, u32[]{:S(2)}) collective-permute-start(f32[8,264,128]{2,1,0:T(8,128)S(1)} %get-tuple-element.8), channel_id=1, source_target_pairs={{0,32},{32,0},{1,33},{33,1},{2,34},{34,2},{3,35},{35,3},{4,36},{36... | collective-permute-start | bytes 3244040 | tf_op jit(solution)/shard_map/ppermute | solution.py:138
  12.8 2.3 %collective-permute-done = f32[8,264,128]{2,1,0:T(8,128)S(1)} collective-permute-done((f32[8,264,128]{2,1,0:T(8,128)S(1)}, f32[8,264,128]{2,1,0:T(8,128)S(1)}, u32[]{:S(2)}, u32[]{:S(2)}) %collective-permute-start) | collective-permute-done | bytes 1081376 | tf_op jit(solution)/shard_map/ppermute | solution.py:138
  15.1 0.9 slice_add_fusion.1
  16.0 11.7 %all_to_all.25 = f32[4,264,128]{2,1,0:T(8,128)S(1)} all-to-all(f32[4,264,128]{2,1,0:T(8,128)S(1)} %get-tuple-element.10), channel_id=1, replica_groups=mesh['y'=4,'zh'=2,'c'=2,'zl'=8,'x'=4] {'y'}, dimensions={0} | all-to-all | bytes 1081344 | tf_op jit(solution)/shard_map/all_to_all | solution.py:142
  27.7 3.6 %all-to-all-start = ((f32[4,264,128]{2,1,0:T(8,128)}), f32[4,264,128]{2,1,0:T(8,128)S(1)}, u32[]{:S(2)}, u32[]{:S(2)}) async-start(f32[4,264,128]{2,1,0:T(8,128)} %get-tuple-element.9), calls=%async_computation | async-start | bytes 1081344 | tf_op jit(solution)/shard_map/all_to_all | solution.py:142
  31.4 11.4 %collective-permute-start.2 = (f32[264,128]{1,0:T(8,128)S(1)}, f32[264,128]{1,0:T(8,128)S(1)}, u32[]{:S(2)}, u32[]{:S(2)}) collective-permute-start(f32[264,128]{1,0:T(8,128)S(1)} %reduce_sum.19.own_ref), channel_id=1, source_target_pairs={{0,64},{64,0},{1,65},{65,1},{2,66},{66,2},{3,67},{67,3},{4,68},{68... | collective-permute-start | bytes 405512 | tf_op jit(solution)/shard_map/ppermute | solution.py:144
  42.8 0.0 all-to-all-done
  42.9 0.6 broadcast_in_dim.8
  43.5 10.7 %all-to-all-start.1 = ((f32[64,1,128]{2,1,0:T(1,128)}), f32[64,1,128]{2,1,0:T(1,128)S(1)}, u32[]{:S(2)}, u32[]{:S(2)}) async-start(f32[64,1,128]{2,1,0:T(1,128)} %broadcast_in_dim.8), calls=%async_computation.1 | async-start | bytes 65536 | tf_op jit(solution)/shard_map/all_to_all | solution.py:146
  54.2 11.7 %collective-permute-start.1 = (f32[264,128]{1,0:T(8,128)S(1)}, f32[264,128]{1,0:T(8,128)S(1)}, u32[]{:S(2)}, u32[]{:S(2)}) collective-permute-start(f32[264,128]{1,0:T(8,128)S(1)} %reduce_sum.18.own_ref), channel_id=1, source_target_pairs={{0,64},{64,0},{1,65},{65,1},{2,66},{66,2},{3,67},{67,3},{4,68},{68... | collective-permute-start | bytes 405512 | tf_op jit(solution)/shard_map/ppermute | solution.py:144
  65.9 0.1 pad_add_fusion.2.where_ref
  66.0 1.6 %all-to-all-done.1 = f32[64,1,128]{2,1,0:T(1,128)S(1)} async-done(((f32[64,1,128]{2,1,0:T(1,128)}), f32[64,1,128]{2,1,0:T(1,128)S(1)}, u32[]{:S(2)}, u32[]{:S(2)}) %all-to-all-start.1) | async-done | bytes 32800 | tf_op jit(solution)/shard_map/all_to_all | solution.py:146
  67.6 0.0 collective-permute-done.2.other_ref
  67.6 9.3 %solve.3 = f32[8,16,256]{2,1,0:T(8,128)} custom-call(s32[2]{0:T(128)S(1)} %pad_add_fusion.2.where_ref, s32[512]{0:T(512)S(1)} %copy-done.2, s32[4,128]{1,0:T(4,128)S(1)} %bitcast.16, f32[264,128]{1,0:T(8,128)S(1)} %reduce_sum.19.own_ref, f32[264,128]{1,0:T(8,128)S(1)} %collective-permute-done.2.other_ref, f32[64,128]{1,0:T(8,128)S(1)} %bitcast.14), custom_call_target="tpu_custom_call" | custom-call | tf_op jit(solution)/shard_map/solve/pallas_call | solution.py:150
  76.9 7.7 %all-to-all-start.4 = ((f32[8,16,256]{2,1,0:T(8,128)}), f32[8,16,256]{2,1,0:T(8,128)S(1)}, u32[]{:S(2)}, u32[]{:S(2)}) async-start(f32[8,16,256]{2,1,0:T(8,128)} %solve.3), calls=%async_computation.4 | async-start | bytes 262144 | tf_op jit(solution)/shard_map/all_to_all | solution.py:159
  84.6 0.1 pad_add_fusion.where_ref
  84.7 0.0 collective-permute-done.1.other_ref
  84.7 8.6 %solve.2 = f32[8,16,256]{2,1,0:T(8,128)S(1)} custom-call(s32[2]{0:T(128)S(1)} %pad_add_fusion.where_ref, s32[512]{0:T(512)S(1)} %copy-done.2, s32[4,128]{1,0:T(4,128)S(1)} %bitcast.17, f32[264,128]{1,0:T(8,128)S(1)} %reduce_sum.18.own_ref, f32[264,128]{1,0:T(8,128)S(1)} %collective-permute-done.1.other_ref, f32[64,128]{1,0:T(8,128)S(1)} %bitcast.15), custom_call_target="tpu_custom_call" | custom-call | tf_op jit(solution)/shard_map/solve/pallas_call | solution.py:150
  93.4 9.8 %all_to_all.26 = f32[8,16,256]{2,1,0:T(8,128)S(1)} all-to-all(f32[8,16,256]{2,1,0:T(8,128)S(1)} %solve.2), channel_id=1, replica_groups=mesh['y'=4,'zh'=2,'c'=2,'zl'=8,'x'=4] {'c','y'}, dimensions={0} | all-to-all | bytes 262144 | tf_op jit(solution)/shard_map/all_to_all | solution.py:159
  103.2 0.7 copy.4
  (9 shorter events, 0.1 us)
Async XLA Ops:
  0.1 1.6 %copy-start = (bf16[1,16,1,256,256]{4,3,2,1,0:T(8,128)(2,1)S(1)}, bf16[1,16,1,256,256]{4,3,2,1,0:T(8,128)(2,1)}, u32[]{:S(2)}) copy-start(bf16[1,16,1,256,256]{4,3,2,1,0:T(8,128)(2,1)} %param.2) | copy-start | bytes 6291460
  1.7 0.7 copy-start.1
  4.0 11.1 %collective-permute-start = (f32[8,264,128]{2,1,0:T(8,128)S(1)}, f32[8,264,128]{2,1,0:T(8,128)S(1)}, u32[]{:S(2)}, u32[]{:S(2)}) collective-permute-start(f32[8,264,128]{2,1,0:T(8,128)S(1)} %get-tuple-element.8), channel_id=1, source_target_pairs={{0,32},{32,0},{1,33},{33,1},{2,34},{34,2},{3,35},{35,3},{4,36},{36... | collective-permute-start | bytes 3244040 | tf_op jit(solution)/shard_map/ppermute | solution.py:138
  27.7 39.9 %copy-start.2 = (s32[512]{0:T(512)S(1)}, s32[512]{0:T(512)}, u32[]{:S(2)}) copy-start(s32[512]{0:T(512)} %layers_ref.5) | copy-start | bytes 6148
  27.7 15.1 %all-to-all-start = ((f32[4,264,128]{2,1,0:T(8,128)}), f32[4,264,128]{2,1,0:T(8,128)S(1)}, u32[]{:S(2)}, u32[]{:S(2)}) async-start(f32[4,264,128]{2,1,0:T(8,128)} %get-tuple-element.9), calls=%async_computation | async-start | bytes 1081344 | tf_op jit(solution)/shard_map/all_to_all | solution.py:142
  31.4 36.2 %collective-permute-start.2 = (f32[264,128]{1,0:T(8,128)S(1)}, f32[264,128]{1,0:T(8,128)S(1)}, u32[]{:S(2)}, u32[]{:S(2)}) collective-permute-start(f32[264,128]{1,0:T(8,128)S(1)} %reduce_sum.19.own_ref), channel_id=1, source_target_pairs={{0,64},{64,0},{1,65},{65,1},{2,66},{66,2},{3,67},{67,3},{4,68},{68... | collective-permute-start | bytes 405512 | tf_op jit(solution)/shard_map/ppermute | solution.py:144
  43.5 24.1 %all-to-all-start.1 = ((f32[64,1,128]{2,1,0:T(1,128)}), f32[64,1,128]{2,1,0:T(1,128)S(1)}, u32[]{:S(2)}, u32[]{:S(2)}) async-start(f32[64,1,128]{2,1,0:T(1,128)} %broadcast_in_dim.8), calls=%async_computation.1 | async-start | bytes 65536 | tf_op jit(solution)/shard_map/all_to_all | solution.py:146
  54.2 30.5 %collective-permute-start.1 = (f32[264,128]{1,0:T(8,128)S(1)}, f32[264,128]{1,0:T(8,128)S(1)}, u32[]{:S(2)}, u32[]{:S(2)}) collective-permute-start(f32[264,128]{1,0:T(8,128)S(1)} %reduce_sum.18.own_ref), channel_id=1, source_target_pairs={{0,64},{64,0},{1,65},{65,1},{2,66},{66,2},{3,67},{67,3},{4,68},{68... | collective-permute-start | bytes 405512 | tf_op jit(solution)/shard_map/ppermute | solution.py:144
  76.9 16.5 %all-to-all-start.4 = ((f32[8,16,256]{2,1,0:T(8,128)}), f32[8,16,256]{2,1,0:T(8,128)S(1)}, u32[]{:S(2)}, u32[]{:S(2)}) async-start(f32[8,16,256]{2,1,0:T(8,128)} %solve.3), calls=%async_computation.4 | async-start | bytes 262144 | tf_op jit(solution)/shard_map/all_to_all | solution.py:159

commit v3 on v1

v3 whole, which is shorter than its diff:
```python
import jax
import jax.numpy as jnp
from jax import lax
from jax.experimental import pallas as pl
from jax.experimental.pallas import tpu as pltpu
from jax.sharding import Mesh
from jax.sharding import PartitionSpec as P

ITERS = 8
FULL_STEPS = 1
ORDER = 256
HALF = 128
ROWS = 520
TAIL = 512
DP = ("y", "zh", "c")
MP = ("zl", "x")


def _iotas(shape):
    return lax.broadcasted_iota(jnp.int32, shape, 0), lax.broadcasted_iota(jnp.int32, shape, 1)


def _nt(a, b):
    return lax.dot_general(a, b, (((1,), (1,)), ((), ())), preferred_element_type=jnp.float32)


def _stats_kernel(where_ref, layers_hbm, grad_hbm, send_ref, own_ref, grad_ref, layers_ref, sems):
    core, holder, holders = where_ref[0], where_ref[1], 32
    blocks = grad_ref.shape[0]
    half, group = blocks // 2, 2
    layers_copy = pltpu.make_async_copy(layers_hbm, layers_ref, sems.at[blocks // group])
    layers_copy.start()
    copies = []
    for n in range(blocks // group):
        first = jnp.where(n * group < half, (1 - core) * half, (core - 1) * half) + n * group
        copies.append(pltpu.make_async_copy(grad_hbm.at[pl.ds(first, group)], grad_ref.at[pl.ds(n * group, group)], sems.at[n]))
        copies[n].start()
    row, col = _iotas((HALF, HALF))
    on = row == col
    lane = lax.broadcasted_iota(jnp.int32, (1, HALF), 1)
    diagonals, traces = [], []
    for n in range(blocks):
        if n % group == 0:
            copies[n // group].wait()
        out_ref, place = (send_ref, n) if n < half else (own_ref, n - half)
        line, start = place // 2, (place % 2) * 2 * HALF
        gradient = grad_ref[n]
        top = _nt(gradient[:HALF], gradient)
        low = _nt(gradient[HALF:], gradient[HALF:])
        left = top[:, :HALF]
        out_ref[line, start : start + HALF, :] = top[:, HALF:]
        out_ref[line, start + HALF : start + 2 * HALF, :] = jnp.where(row > col, left, low)
        diag_left = jnp.sum(jnp.where(on, left, 0.0), axis=0, keepdims=True)
        diag_low = jnp.sum(jnp.where(on, low, 0.0), axis=0, keepdims=True)
        diagonals.append(diag_left)
        traces.append(jnp.sum(diag_left + diag_low, axis=1, keepdims=True))
    layers_copy.wait()
    sums = jnp.zeros((1, HALF), jnp.float32)
    for n in range(blocks):
        block = n + ((1 - core) * half if n < half else (core - 1) * half)
        sums = sums + jnp.where(lane == layers_ref[block * holders + holder], traces[n], 0.0)
    tail_row, _ = _iotas((8, HALF))
    for n in range(0, blocks, 2):
        out_ref, line = (send_ref, n // 2) if n < half else (own_ref, (n - half) // 2)
        tail = jnp.where(tail_row == 1, diagonals[n + 1], jnp.where(tail_row == 2, sums, 0.0))
        out_ref[line, TAIL:, :] = jnp.where(tail_row == 0, diagonals[n], tail)


def _split(a):
    high = a.astype(jnp.bfloat16)
    return high, (a - high.astype(jnp.float32)).astype(jnp.bfloat16)


def _dot(a, b):
    return jnp.dot(a, b, preferred_element_type=jnp.float32)


def _product(a, b):
    return _dot(a[0], b[0]) + (_dot(a[0], b[1]) + _dot(a[1], b[0]))


def _full(a, b):
    return jnp.dot(a, b, precision=lax.Precision.HIGHEST, preferred_element_type=jnp.float32)


def _unpack(corner, both, diagonal):
    row, col = _iotas((HALF, HALF))
    flipped = both.T
    left = jnp.where(row > col, both, jnp.where(row < col, flipped, diagonal))
    low = jnp.where(row <= col, both, flipped)
    return jnp.concatenate([jnp.concatenate([left, corner], 1), jnp.concatenate([corner.T, low], 1)], 0)


def _factor(on, coupled):
    return jnp.where(on, 1.25, 0.0) - 0.25 * coupled


def _solve_kernel(where_ref, layers_ref, map_ref, own_ref, other_ref, sums_ref, out_ref, first_ref):
    core, line, side, holder = where_ref[0], where_ref[1], where_ref[2], where_ref[3]
    pair = range(2)
    row, col = _iotas((ORDER, ORDER))
    on = row == col
    lane = lax.broadcasted_iota(jnp.int32, (1, HALF), 1)
    totals = jnp.sum(sums_ref[...], axis=0, keepdims=True) * (1.0 / 4096.0)
    coupled, factor, current = [], [], []
    for k in pair:
        corner, both, diagonal = (
            (own_ref[rows, :] + other_ref[rows, :]) * (1.0 / 4096.0)
            for rows in (
                slice(k * 2 * HALF, k * 2 * HALF + HALF),
                slice(k * 2 * HALF + HALF, (k + 1) * 2 * HALF),
                slice(TAIL + k, TAIL + k + 1),
            )
        )
        layer = layers_ref[((core * 4 + line) * 2 + k) * 32 + holder]
        members = jnp.sum(jnp.where(map_ref[...] == layer, 1.0, 0.0), axis=(0, 1), keepdims=True)
        total = jnp.sum(jnp.where(lane == layer, totals, 0.0), axis=1, keepdims=True)
        damped = _unpack(corner, both, diagonal) + jnp.where(on, 0.1 * total / (members * ORDER), 0.0)
        scaled = 2.5 / jnp.sqrt(jnp.sum(damped * damped, axis=(0, 1), keepdims=True))
        coupled.append(scaled * damped)
        factor.append(_factor(on, coupled[k]))
        first_ref[k] = jnp.sqrt(jnp.sqrt(scaled)) * factor[k]
        current.append(jnp.concatenate([first_ref[k, pl.ds(q * 64 + side * 32, 32), :] for q in range(4)], 0))
    for step in range(ITERS - 1):
        if step < FULL_STEPS:
            square = [_full(factor[k], factor[k]) for k in pair]
            fourth = [_full(square[k], square[k]) for k in pair]
            coupled = [_full(fourth[k], coupled[k]) for k in pair]
        else:
            parts = [_split(factor[k]) for k in pair]
            square = [_split(_product(parts[k], parts[k])) for k in pair]
            fourth = [_split(_product(square[k], square[k])) for k in pair]
            coupled = [_product(fourth[k], _split(coupled[k])) for k in pair]
        factor = [_factor(on, coupled[k]) for k in pair]
        current = [_product(_split(current[k]), _split(factor[k])) for k in pair]
    for k in pair:
        for c in range(2):
            for q in range(4):
                out_ref[c * 4 + q, k] = current[k][(q * 2 + c) * 16 : (q * 2 + c) * 16 + 16]


def _smem():
    return pl.BlockSpec(memory_space=pltpu.SMEM)


def _hbm():
    return pl.BlockSpec(memory_space=pltpu.HBM)


def _vmem():
    return pl.BlockSpec(memory_space=pltpu.VMEM)


def local(grads, layer_map):
    gradient = grads[0, :, 0]
    core, line, side = lax.axis_index("c"), lax.axis_index("y"), lax.axis_index("zh")
    holder = lax.axis_index(MP)
    half = gradient.shape[0] // 2
    pack = jax.ShapeDtypeStruct((half // 2, ROWS, HALF), jnp.float32)
    send, own = pl.pallas_call(
        _stats_kernel,
        out_shape=(pack, pack),
        in_specs=[_smem(), _hbm(), _hbm()],
        out_specs=(_vmem(), _vmem()),
        scratch_shapes=[
            pltpu.VMEM(gradient.shape, gradient.dtype),
            pltpu.SMEM(layer_map.shape, layer_map.dtype),
            pltpu.SemaphoreType.DMA((gradient.shape[0] // 2 + 1,)),
        ],
        compiler_params=pltpu.CompilerParams(vmem_limit_bytes=52000 * 2**10),
        name="stats",
    )(jnp.stack([core, holder]).astype(jnp.int32), layer_map, gradient)
    got = lax.ppermute(send, "c", [(0, 1), (1, 0)])
    chip = own + got
    pieces = lax.all_to_all(chip, "y", 0, 0, tiled=True)
    mine = jnp.sum(pieces, axis=0)
    other = lax.ppermute(mine, "zh", [(0, 1), (1, 0)])
    row = jnp.broadcast_to(mine[TAIL + 2][None, None], (64, 1, HALF))
    sums = lax.all_to_all(row, ("zh", "zl", "x"), 0, 0, tiled=True)
    rows = pl.pallas_call(
        _solve_kernel,
        out_shape=jax.ShapeDtypeStruct((8, half // 4, 16, ORDER), jnp.float32),
        in_specs=[_smem(), _smem(), _vmem(), _vmem(), _vmem(), _vmem()],
        out_specs=_vmem(),
        scratch_shapes=[pltpu.VMEM((half // 4, ORDER, ORDER), jnp.float32)],
        compiler_params=pltpu.CompilerParams(vmem_limit_bytes=16 * 2**20),
        name="solve",
    )(
        jnp.stack([core, line, side, holder]).astype(jnp.int32),
        layer_map,
        layer_map.reshape(4, HALF),
        mine,
        other,
        sums.reshape(64, HALF),
    )
    back = lax.all_to_all(rows, ("c", "y"), 0, 0, tiled=True)
    return back.reshape(16, 1, 16, ORDER)


def solution(mesh):
    torus = Mesh(mesh.devices.reshape(4, 2, 2, 8, 4), ("y", "zh", "c", "zl", "x"))
    in_specs = (P(DP, None, MP, None, None), P())
    out_specs = P(None, MP, DP, None)
    return jax.shard_map(local, mesh=torus, in_specs=in_specs, out_specs=out_specs, check_vma=False)
```

time: 100 us -> 98.5 us (0.985)
  local copies, waits for them, and re-layouts: 3.61 us -> 2.02 us
    pallas_call x1, Pallas kernels: 1.66 us -> 4.29 us  [local(): pl.pallas_call(_stats_kernel, out_shape=(pack, pack), in_specs=[_smem(),...]
    pallas_call x1, Pallas kernels: 11.2 us -> 9.17 us  [local(): pl.pallas_call(_solve_kernel, out_shape=jax.ShapeDtypeStruct((8, half //...]
    unnamed x7 -> x5, local copies, waits for them, and re-layouts: 2.98 us -> 1.39 us
where the time goes in v3:
time: 98.5 us; the launch traced here: 98.2 us
  blocking collectives  28.9 us (29%)
  starting transfers between devices  28.4 us (29%)
  waiting for transfers between devices  25 us (25%)
  Pallas kernels  13.5 us (14%)
  local copies, waits for them, and re-layouts  2.02 us (2%)
    all_to_all x1, waiting for transfers between devices, local(): sums = lax.all_to_all(row, ('zh', 'zl', 'x'), 0, 0, tiled=True)  22.7 us
    all_to_all x1, blocking collectives, local(): pieces = lax.all_to_all(chip, 'y', 0, 0, tiled=True)  17.4 us
    all_to_all x1, blocking collectives, local(): back = lax.all_to_all(rows, ('c', 'y'), 0, 0, tiled=True)  11.5 us
    ppermute x1, starting transfers between devices, local(): other = lax.ppermute(mine, 'zh', [(0, 1), (1, 0)])  11.4 us
    pallas_call x1, Pallas kernels, local(): pl.pallas_call(_solve_kernel, out_shape=jax.ShapeDtypeStruct((8, half //...  9.17 us
    ppermute x1, starting transfers between devices, local(): got = lax.ppermute(send, 'c', [(0, 1), (1, 0)])  8.75 us
    all_to_all x1, starting transfers between devices, local(): sums = lax.all_to_all(row, ('zh', 'zl', 'x'), 0, 0, tiled=True)  8.21 us
    pallas_call x1, Pallas kernels, local(): pl.pallas_call(_stats_kernel, out_shape=(pack, pack), in_specs=[_smem(),...  4.29 us
  transfers between devices with their start and end apart: 3, of which 2 were waited for; matrix products, arithmetic and copies ran while one was open for 1% of the time, Pallas kernels for 0%

profile of v3, /device:TPU:1, one launch (start us, length us, event | category | flops | bytes accessed | tf_op | source)
XLA Modules:
  0.0 98.2 jit_solution(14556569345736278828)
XLA Ops:
  0.0 0.1 pad_add_fusion.1.where_ref
  0.1 0.0 copy-start
  0.1 0.7 copy-done
  0.8 4.3 %stats.1 = (f32[4,520,128]{2,1,0:T(8,128)S(1)}, f32[4,520,128]{2,1,0:T(8,128)S(1)}) custom-call(s32[2]{0:T(128)S(1)} %pad_add_fusion.1.where_ref, s32[512]{0:T(512)S(1)} %copy-done, bf16[16,256,256]{2,1,0:T(8,128)(2,1)} %bitcast.14), custom_call_target="tpu_custom_call" | custom-call | tf_op jit(solution)/shard_map/stats/pallas_call | solution.py:160
  5.1 8.7 %collective-permute-start = (f32[4,520,128]{2,1,0:T(8,128)S(1)}, f32[4,520,128]{2,1,0:T(8,128)S(1)}, u32[]{:S(2)}, u32[]{:S(2)}) collective-permute-start(f32[4,520,128]{2,1,0:T(8,128)S(1)} %get-tuple-element.8), channel_id=1, source_target_pairs={{0,32},{32,0},{1,33},{33,1},{2,34},{34,2},{3,35},{35,3},{4,36},{36... | collective-permute-start | bytes 3194888 | tf_op jit(solution)/shard_map/ppermute | solution.py:173
  13.8 2.3 %collective-permute-done = f32[4,520,128]{2,1,0:T(8,128)S(1)} collective-permute-done((f32[4,520,128]{2,1,0:T(8,128)S(1)}, f32[4,520,128]{2,1,0:T(8,128)S(1)}, u32[]{:S(2)}, u32[]{:S(2)}) %collective-permute-start) | collective-permute-done | bytes 1064992 | tf_op jit(solution)/shard_map/ppermute | solution.py:173
  16.1 0.1 add.7
  16.2 17.4 %all_to_all.15 = f32[4,520,128]{2,1,0:T(8,128)S(1)} all-to-all(f32[4,520,128]{2,1,0:T(8,128)S(1)} %add.7), channel_id=1, replica_groups=mesh['y'=4,'zh'=2,'c'=2,'zl'=8,'x'=4] {'y'}, dimensions={0} | all-to-all | bytes 2129920 | tf_op jit(solution)/shard_map/all_to_all | solution.py:175
  33.6 0.0 copy-start.1
  33.6 0.1 reduce_sum.9.own_ref
  33.7 11.4 %collective-permute-start.1 = (f32[520,128]{1,0:T(8,128)S(1)}, f32[520,128]{1,0:T(8,128)S(1)}, u32[]{:S(2)}, u32[]{:S(2)}) collective-permute-start(f32[520,128]{1,0:T(8,128)S(1)} %reduce_sum.9.own_ref), channel_id=1, source_target_pairs={{0,64},{64,0},{1,65},{65,1},{2,66},{66,2},{3,67},{67,3},{4,68},{68... | collective-permute-start | bytes 798728 | tf_op jit(solution)/shard_map/ppermute | solution.py:177
  45.1 0.6 broadcast_in_dim.8
  45.8 8.2 %all-to-all-start.1 = ((f32[64,1,128]{2,1,0:T(1,128)}), f32[64,1,128]{2,1,0:T(1,128)S(1)}, u32[]{:S(2)}, u32[]{:S(2)}) async-start(f32[64,1,128]{2,1,0:T(1,128)} %broadcast_in_dim.8), calls=%async_computation.1 | async-start | bytes 65536 | tf_op jit(solution)/shard_map/all_to_all | solution.py:179
  54.0 0.1 pad_add_fusion.where_ref
  54.1 22.7 %all-to-all-done.1 = f32[64,1,128]{2,1,0:T(1,128)S(1)} async-done(((f32[64,1,128]{2,1,0:T(1,128)}), f32[64,1,128]{2,1,0:T(1,128)S(1)}, u32[]{:S(2)}, u32[]{:S(2)}) %all-to-all-start.1) | async-done | bytes 32800 | tf_op jit(solution)/shard_map/all_to_all | solution.py:179
  76.8 0.0 collective-permute-done.1.other_ref
  76.8 0.0 copy-done.1
  76.8 9.2 %solve.1 = f32[8,2,16,256]{3,2,1,0:T(8,128)S(1)} custom-call(s32[4]{0:T(128)S(1)} %pad_add_fusion.where_ref, s32[512]{0:T(512)S(1)} %copy-done.1, s32[4,128]{1,0:T(4,128)S(1)} %bitcast.13, f32[520,128]{1,0:T(8,128)S(1)} %reduce_sum.9.own_ref, f32[520,128]{1,0:T(8,128)S(1)} %collective-permute-done.1.other_ref, f32[64,128]{1,0:T(8,128)S(1)} %bitcast.12), custom_call_target="tpu_custom_call" | custom-call | tf_op jit(solution)/shard_map/solve/pallas_call | solution.py:180
  85.9 11.5 %all_to_all.16 = f32[8,2,16,256]{3,2,1,0:T(8,128)S(1)} all-to-all(f32[8,2,16,256]{3,2,1,0:T(8,128)S(1)} %solve.1), channel_id=1, replica_groups=mesh['y'=4,'zh'=2,'c'=2,'zl'=8,'x'=4] {'c','y'}, dimensions={0} | all-to-all | bytes 524288 | tf_op jit(solution)/shard_map/all_to_all | solution.py:196
  97.5 0.7 copy.6
  (1 shorter events, 0.0 us)
Async XLA Ops:
  0.1 0.7 copy-start
  5.1 11.0 %collective-permute-start = (f32[4,520,128]{2,1,0:T(8,128)S(1)}, f32[4,520,128]{2,1,0:T(8,128)S(1)}, u32[]{:S(2)}, u32[]{:S(2)}) collective-permute-start(f32[4,520,128]{2,1,0:T(8,128)S(1)} %get-tuple-element.8), channel_id=1, source_target_pairs={{0,32},{32,0},{1,33},{33,1},{2,34},{34,2},{3,35},{35,3},{4,36},{36... | collective-permute-start | bytes 3194888 | tf_op jit(solution)/shard_map/ppermute | solution.py:173
  33.6 43.1 %copy-start.1 = (s32[512]{0:T(512)S(1)}, s32[512]{0:T(512)}, u32[]{:S(2)}) copy-start(s32[512]{0:T(512)} %layers_ref.1) | copy-start | bytes 6148
  33.7 43.0 %collective-permute-start.1 = (f32[520,128]{1,0:T(8,128)S(1)}, f32[520,128]{1,0:T(8,128)S(1)}, u32[]{:S(2)}, u32[]{:S(2)}) collective-permute-start(f32[520,128]{1,0:T(8,128)S(1)} %reduce_sum.9.own_ref), channel_id=1, source_target_pairs={{0,64},{64,0},{1,65},{65,1},{2,66},{66,2},{3,67},{67,3},{4,68},{68... | collective-permute-start | bytes 798728 | tf_op jit(solution)/shard_map/ppermute | solution.py:177
  45.8 31.0 %all-to-all-start.1 = ((f32[64,1,128]{2,1,0:T(1,128)}), f32[64,1,128]{2,1,0:T(1,128)S(1)}, u32[]{:S(2)}, u32[]{:S(2)}) async-start(f32[64,1,128]{2,1,0:T(1,128)} %broadcast_in_dim.8), calls=%async_computation.1 | async-start | bytes 65536 | tf_op jit(solution)/shard_map/all_to_all | solution.py:179

commit v4 on v3

--- a/solution.py
+++ b/solution.py
@@ -24,27 +24,19 @@
     return lax.dot_general(a, b, (((1,), (1,)), ((), ())), preferred_element_type=jnp.float32)
 
 
-def _stats_kernel(where_ref, layers_hbm, grad_hbm, send_ref, own_ref, grad_ref, layers_ref, sems):
-    core, holder, holders = where_ref[0], where_ref[1], 32
+def _stats_kernel(where_ref, grad_ref, send_ref, own_ref):
+    core = where_ref[0]
     blocks = grad_ref.shape[0]
-    half, group = blocks // 2, 2
-    layers_copy = pltpu.make_async_copy(layers_hbm, layers_ref, sems.at[blocks // group])
-    layers_copy.start()
-    copies = []
-    for n in range(blocks // group):
-        first = jnp.where(n * group < half, (1 - core) * half, (core - 1) * half) + n * group
-        copies.append(pltpu.make_async_copy(grad_hbm.at[pl.ds(first, group)], grad_ref.at[pl.ds(n * group, group)], sems.at[n]))
-        copies[n].start()
+    half = blocks // 2
     row, col = _iotas((HALF, HALF))
     on = row == col
     lane = lax.broadcasted_iota(jnp.int32, (1, HALF), 1)
-    diagonals, traces = [], []
+    diagonals, traces = [], jnp.zeros((1, HALF), jnp.float32)
     for n in range(blocks):
-        if n % group == 0:
-            copies[n // group].wait()
         out_ref, place = (send_ref, n) if n < half else (own_ref, n - half)
         line, start = place // 2, (place % 2) * 2 * HALF
-        gradient = grad_ref[n]
+        block = n + ((1 - core) * half if n < half else (core - 1) * half)
+        gradient = grad_ref[block]
         top = _nt(gradient[:HALF], gradient)
         low = _nt(gradient[HALF:], gradient[HALF:])
         left = top[:, :HALF]
@@ -53,16 +45,11 @@
         diag_left = jnp.sum(jnp.where(on, left, 0.0), axis=0, keepdims=True)
         diag_low = jnp.sum(jnp.where(on, low, 0.0), axis=0, keepdims=True)
         diagonals.append(diag_left)
-        traces.append(jnp.sum(diag_left + diag_low, axis=1, keepdims=True))
-    layers_copy.wait()
-    sums = jnp.zeros((1, HALF), jnp.float32)
-    for n in range(blocks):
-        block = n + ((1 - core) * half if n < half else (core - 1) * half)
-        sums = sums + jnp.where(lane == layers_ref[block * holders + holder], traces[n], 0.0)
+        traces = traces + jnp.where(lane == block, jnp.sum(diag_left + diag_low, axis=1, keepdims=True), 0.0)
     tail_row, _ = _iotas((8, HALF))
     for n in range(0, blocks, 2):
         out_ref, line = (send_ref, n // 2) if n < half else (own_ref, (n - half) // 2)
-        tail = jnp.where(tail_row == 1, diagonals[n + 1], jnp.where(tail_row == 2, sums, 0.0))
+        tail = jnp.where(tail_row == 1, diagonals[n + 1], jnp.where(tail_row == 2, traces, 0.0))
         out_ref[line, TAIL:, :] = jnp.where(tail_row == 0, diagonals[n], tail)
 
 
@@ -95,13 +82,11 @@
     return jnp.where(on, 1.25, 0.0) - 0.25 * coupled
 
 
-def _solve_kernel(where_ref, layers_ref, map_ref, own_ref, other_ref, sums_ref, out_ref, first_ref):
-    core, line, side, holder = where_ref[0], where_ref[1], where_ref[2], where_ref[3]
+def _solve_kernel(where_ref, map_ref, own_ref, other_ref, traces_ref, out_ref, first_ref):
+    side = where_ref[0]
     pair = range(2)
     row, col = _iotas((ORDER, ORDER))
     on = row == col
-    lane = lax.broadcasted_iota(jnp.int32, (1, HALF), 1)
-    totals = jnp.sum(sums_ref[...], axis=0, keepdims=True) * (1.0 / 4096.0)
     coupled, factor, current = [], [], []
     for k in pair:
         corner, both, diagonal = (
@@ -112,9 +97,9 @@
                 slice(TAIL + k, TAIL + k + 1),
             )
         )
-        layer = layers_ref[((core * 4 + line) * 2 + k) * 32 + holder]
-        members = jnp.sum(jnp.where(map_ref[...] == layer, 1.0, 0.0), axis=(0, 1), keepdims=True)
-        total = jnp.sum(jnp.where(lane == layer, totals, 0.0), axis=1, keepdims=True)
+        held = map_ref[...] == where_ref[1 + k]
+        members = jnp.sum(jnp.where(held, 0.5, 0.0), axis=(0, 1), keepdims=True)
+        total = jnp.sum(jnp.where(held, traces_ref[...], 0.0), axis=(0, 1), keepdims=True) * (1.0 / 4096.0)
         damped = _unpack(corner, both, diagonal) + jnp.where(on, 0.1 * total / (members * ORDER), 0.0)
         scaled = 2.5 / jnp.sqrt(jnp.sum(damped * damped, axis=(0, 1), keepdims=True))
         coupled.append(scaled * damped)
@@ -143,10 +128,6 @@
     return pl.BlockSpec(memory_space=pltpu.SMEM)
 
 
-def _hbm():
-    return pl.BlockSpec(memory_space=pltpu.HBM)
-
-
 def _vmem():
     return pl.BlockSpec(memory_space=pltpu.VMEM)
 
@@ -160,39 +141,31 @@
     send, own = pl.pallas_call(
         _stats_kernel,
         out_shape=(pack, pack),
-        in_specs=[_smem(), _hbm(), _hbm()],
+        in_specs=[_smem(), _vmem()],
         out_specs=(_vmem(), _vmem()),
-        scratch_shapes=[
-            pltpu.VMEM(gradient.shape, gradient.dtype),
-            pltpu.SMEM(layer_map.shape, layer_map.dtype),
-            pltpu.SemaphoreType.DMA((gradient.shape[0] // 2 + 1,)),
-        ],
-        compiler_params=pltpu.CompilerParams(vmem_limit_bytes=52000 * 2**10),
+        compiler_params=pltpu.CompilerParams(vmem_limit_bytes=16 * 2**20),
         name="stats",
-    )(jnp.stack([core, holder]).astype(jnp.int32), layer_map, gradient)
+    )(core.astype(jnp.int32).reshape(1), gradient)
     got = lax.ppermute(send, "c", [(0, 1), (1, 0)])
     chip = own + got
     pieces = lax.all_to_all(chip, "y", 0, 0, tiled=True)
     mine = jnp.sum(pieces, axis=0)
     other = lax.ppermute(mine, "zh", [(0, 1), (1, 0)])
     row = jnp.broadcast_to(mine[TAIL + 2][None, None], (64, 1, HALF))
-    sums = lax.all_to_all(row, ("zh", "zl", "x"), 0, 0, tiled=True)
+    traces = lax.all_to_all(row, ("zh", "zl", "x"), 0, 0, tiled=True).reshape(64, HALF)
+    layers = layer_map.reshape(2 * half, 32)
+    layer_of = jnp.pad(jnp.tile(layers.T, (2, 1)), ((0, 0), (0, HALF - 2 * half)), constant_values=-1)
+    block = core * half + line * 2
+    pair = lax.dynamic_slice(layers, (block, holder), (2, 1)).reshape(2)
     rows = pl.pallas_call(
         _solve_kernel,
         out_shape=jax.ShapeDtypeStruct((8, half // 4, 16, ORDER), jnp.float32),
-        in_specs=[_smem(), _smem(), _vmem(), _vmem(), _vmem(), _vmem()],
+        in_specs=[_smem()] + [_vmem()] * 4,
         out_specs=_vmem(),
         scratch_shapes=[pltpu.VMEM((half // 4, ORDER, ORDER), jnp.float32)],
         compiler_params=pltpu.CompilerParams(vmem_limit_bytes=16 * 2**20),
         name="solve",
-    )(
-        jnp.stack([core, line, side, holder]).astype(jnp.int32),
-        layer_map,
-        layer_map.reshape(4, HALF),
-        mine,
-        other,
-        sums.reshape(64, HALF),
-    )
+    )(jnp.concatenate([side.astype(jnp.int32).reshape(1), pair]), layer_of, mine, other, traces)
     back = lax.all_to_all(rows, ("c", "y"), 0, 0, tiled=True)
     return back.reshape(16, 1, 16, ORDER)
 

time: 98.5 us -> 96 us (0.975)
  Pallas kernels: 13.5 us -> 10.2 us
  local copies, waits for them, and re-layouts: 2.02 us -> 3.28 us
    pallas_call x1, Pallas kernels: 4.29 us -> 1.08 us  [local(): pl.pallas_call(_stats_kernel, out_shape=(pack, pack), in_specs=[_smem(),...]
where the time goes in v4:
time: 96 us; the launch traced here: 95.7 us
  blocking collectives  28.9 us (30%)
  starting transfers between devices  28.4 us (30%)
  waiting for transfers between devices  24.6 us (26%)
  Pallas kernels  10.2 us (11%)
  local copies, waits for them, and re-layouts  3.28 us (3%)
    all_to_all x1, waiting for transfers between devices, local(): lax.all_to_all(row, ('zh', 'zl', 'x'), 0, 0, tiled=True).reshape(64, HALF)  22.3 us
    all_to_all x1, blocking collectives, local(): pieces = lax.all_to_all(chip, 'y', 0, 0, tiled=True)  17.4 us
    all_to_all x1, blocking collectives, local(): back = lax.all_to_all(rows, ('c', 'y'), 0, 0, tiled=True)  11.5 us
    ppermute x1, starting transfers between devices, local(): other = lax.ppermute(mine, 'zh', [(0, 1), (1, 0)])  11.4 us
    pallas_call x1, Pallas kernels, local(): pl.pallas_call(_solve_kernel, out_shape=jax.ShapeDtypeStruct((8, half //...  9.12 us
    ppermute x1, starting transfers between devices, local(): got = lax.ppermute(send, 'c', [(0, 1), (1, 0)])  8.74 us
    all_to_all x1, starting transfers between devices, local(): lax.all_to_all(row, ('zh', 'zl', 'x'), 0, 0, tiled=True).reshape(64, HALF)  8.21 us
    unnamed x5, local copies, waits for them, and re-layouts  2.3 us
  transfers between devices with their start and end apart: 3, of which 2 were waited for; matrix products, arithmetic and copies ran while one was open for 1% of the time, Pallas kernels for 0%

profile of v4, /device:TPU:1, one launch (start us, length us, event | category | flops | bytes accessed | tf_op | source)
XLA Modules:
  0.0 95.7 jit_solution(293784165206673074)
XLA Ops:
  0.0 0.0 copy-start
  0.0 1.6 %copy-done = bf16[1,16,1,256,256]{4,3,2,1,0:T(8,128)(2,1)S(1)} copy-done((bf16[1,16,1,256,256]{4,3,2,1,0:T(8,128)(2,1)S(1)}, bf16[1,16,1,256,256]{4,3,2,1,0:T(8,128)(2,1)}, u32[]{:S(2)}) %copy-start) | copy-done | bytes 2097176
  1.6 1.1 %stats.1 = (f32[4,520,128]{2,1,0:T(8,128)S(1)}, f32[4,520,128]{2,1,0:T(8,128)S(1)}) custom-call(s32[1]{0:T(128)} %bitcast.3.where_ref, bf16[16,256,256]{2,1,0:T(8,128)(2,1)S(1)} %bitcast.11), custom_call_target="tpu_custom_call" | custom-call | tf_op jit(solution)/shard_map/stats/pallas_call | solution.py:141
  2.7 8.7 %collective-permute-start = (f32[4,520,128]{2,1,0:T(8,128)S(1)}, f32[4,520,128]{2,1,0:T(8,128)S(1)}, u32[]{:S(2)}, u32[]{:S(2)}) collective-permute-start(f32[4,520,128]{2,1,0:T(8,128)S(1)} %get-tuple-element.8), channel_id=1, source_target_pairs={{0,32},{32,0},{1,33},{33,1},{2,34},{34,2},{3,35},{35,3},{4,36},{36... | collective-permute-start | bytes 3194888 | tf_op jit(solution)/shard_map/ppermute | solution.py:149
  11.4 2.3 %collective-permute-done = f32[4,520,128]{2,1,0:T(8,128)S(1)} collective-permute-done((f32[4,520,128]{2,1,0:T(8,128)S(1)}, f32[4,520,128]{2,1,0:T(8,128)S(1)}, u32[]{:S(2)}, u32[]{:S(2)}) %collective-permute-start) | collective-permute-done | bytes 1064992 | tf_op jit(solution)/shard_map/ppermute | solution.py:149
  13.7 0.1 add.21
  13.8 17.4 %all_to_all.15 = f32[4,520,128]{2,1,0:T(8,128)S(1)} all-to-all(f32[4,520,128]{2,1,0:T(8,128)S(1)} %add.21), channel_id=1, replica_groups=mesh['y'=4,'zh'=2,'c'=2,'zl'=8,'x'=4] {'y'}, dimensions={0} | all-to-all | bytes 2129920 | tf_op jit(solution)/shard_map/all_to_all | solution.py:151
  31.2 0.0 copy-start.1
  31.2 0.1 reduce_sum.9.own_ref
  31.3 11.4 %collective-permute-start.1 = (f32[520,128]{1,0:T(8,128)S(1)}, f32[520,128]{1,0:T(8,128)S(1)}, u32[]{:S(2)}, u32[]{:S(2)}) collective-permute-start(f32[520,128]{1,0:T(8,128)S(1)} %reduce_sum.9.own_ref), channel_id=1, source_target_pairs={{0,64},{64,0},{1,65},{65,1},{2,66},{66,2},{3,67},{67,3},{4,68},{68... | collective-permute-start | bytes 798728 | tf_op jit(solution)/shard_map/ppermute | solution.py:153
  42.7 0.6 broadcast_in_dim.8
  43.3 8.2 %all-to-all-start.1 = ((f32[64,1,128]{2,1,0:T(1,128)}), f32[64,1,128]{2,1,0:T(1,128)S(1)}, u32[]{:S(2)}, u32[]{:S(2)}) async-start(f32[64,1,128]{2,1,0:T(1,128)} %broadcast_in_dim.8), calls=%async_computation.1 | async-start | bytes 65536 | tf_op jit(solution)/shard_map/all_to_all | solution.py:155
  51.6 0.0 copy-done.1
  51.6 0.1 reshape.26
  51.7 0.1 copy.8
  51.7 0.2 dynamic-slice_reduce_fusion
  52.0 0.1 pad_add_fusion.where_ref
  52.0 22.3 %all-to-all-done.1 = f32[64,1,128]{2,1,0:T(1,128)S(1)} async-done(((f32[64,1,128]{2,1,0:T(1,128)}), f32[64,1,128]{2,1,0:T(1,128)S(1)}, u32[]{:S(2)}, u32[]{:S(2)}) %all-to-all-start.1) | async-done | bytes 32800 | tf_op jit(solution)/shard_map/all_to_all | solution.py:155
  74.3 0.0 collective-permute-done.1.other_ref
  74.3 9.1 %solve.1 = f32[8,2,16,256]{3,2,1,0:T(8,128)S(1)} custom-call(s32[3]{0:T(128)S(1)} %pad_add_fusion.where_ref, s32[64,128]{1,0:T(8,128)S(1)} %pad.4.map_ref, f32[520,128]{1,0:T(8,128)S(1)} %reduce_sum.9.own_ref, f32[520,128]{1,0:T(8,128)S(1)} %collective-permute-done.1.other_ref, f32[64,128]{1,0:T(8,128)S(1)} %bitcast.12), custom_call_target="tpu_custom_call" | custom-call | tf_op jit(solution)/shard_map/solve/pallas_call | solution.py:160
  83.5 11.5 %all_to_all.16 = f32[8,2,16,256]{3,2,1,0:T(8,128)S(1)} all-to-all(f32[8,2,16,256]{3,2,1,0:T(8,128)S(1)} %solve.1), channel_id=1, replica_groups=mesh['y'=4,'zh'=2,'c'=2,'zl'=8,'x'=4] {'c','y'}, dimensions={0} | all-to-all | bytes 524288 | tf_op jit(solution)/shard_map/all_to_all | solution.py:169
  95.0 0.7 copy.11
  (3 shorter events, 0.0 us)
Async XLA Ops:
  0.0 1.6 %copy-start = (bf16[1,16,1,256,256]{4,3,2,1,0:T(8,128)(2,1)S(1)}, bf16[1,16,1,256,256]{4,3,2,1,0:T(8,128)(2,1)}, u32[]{:S(2)}) copy-start(bf16[1,16,1,256,256]{4,3,2,1,0:T(8,128)(2,1)} %param.2) | copy-start | bytes 6291460
  2.7 11.0 %collective-permute-start = (f32[4,520,128]{2,1,0:T(8,128)S(1)}, f32[4,520,128]{2,1,0:T(8,128)S(1)}, u32[]{:S(2)}, u32[]{:S(2)}) collective-permute-start(f32[4,520,128]{2,1,0:T(8,128)S(1)} %get-tuple-element.8), channel_id=1, source_target_pairs={{0,32},{32,0},{1,33},{33,1},{2,34},{34,2},{3,35},{35,3},{4,36},{36... | collective-permute-start | bytes 3194888 | tf_op jit(solution)/shard_map/ppermute | solution.py:149
  31.2 20.4 %copy-start.1 = (s32[512]{0:T(512)S(1)}, s32[512]{0:T(512)}, u32[]{:S(2)}) copy-start(s32[512]{0:T(512)} %param.3) | copy-start | bytes 6148
  31.3 43.0 %collective-permute-start.1 = (f32[520,128]{1,0:T(8,128)S(1)}, f32[520,128]{1,0:T(8,128)S(1)}, u32[]{:S(2)}, u32[]{:S(2)}) collective-permute-start(f32[520,128]{1,0:T(8,128)S(1)} %reduce_sum.9.own_ref), channel_id=1, source_target_pairs={{0,64},{64,0},{1,65},{65,1},{2,66},{66,2},{3,67},{67,3},{4,68},{68... | collective-permute-start | bytes 798728 | tf_op jit(solution)/shard_map/ppermute | solution.py:153
  43.3 31.0 %all-to-all-start.1 = ((f32[64,1,128]{2,1,0:T(1,128)}), f32[64,1,128]{2,1,0:T(1,128)S(1)}, u32[]{:S(2)}, u32[]{:S(2)}) async-start(f32[64,1,128]{2,1,0:T(1,128)} %broadcast_in_dim.8), calls=%async_computation.1 | async-start | bytes 65536 | tf_op jit(solution)/shard_map/all_to_all | solution.py:155

commit v5 on v4

--- a/solution.py
+++ b/solution.py
@@ -7,7 +7,6 @@
 from jax.sharding import PartitionSpec as P
 
 ITERS = 8
-FULL_STEPS = 1
 ORDER = 256
 HALF = 128
 ROWS = 520
@@ -66,10 +65,6 @@
     return _dot(a[0], b[0]) + (_dot(a[0], b[1]) + _dot(a[1], b[0]))
 
 
-def _full(a, b):
-    return jnp.dot(a, b, precision=lax.Precision.HIGHEST, preferred_element_type=jnp.float32)
-
-
 def _unpack(corner, both, diagonal):
     row, col = _iotas((HALF, HALF))
     flipped = both.T
@@ -78,16 +73,12 @@
     return jnp.concatenate([jnp.concatenate([left, corner], 1), jnp.concatenate([corner.T, low], 1)], 0)
 
 
-def _factor(on, coupled):
-    return jnp.where(on, 1.25, 0.0) - 0.25 * coupled
-
-
 def _solve_kernel(where_ref, map_ref, own_ref, other_ref, traces_ref, out_ref, first_ref):
     side = where_ref[0]
     pair = range(2)
     row, col = _iotas((ORDER, ORDER))
     on = row == col
-    coupled, factor, current = [], [], []
+    coupled, current = [], []
     for k in pair:
         corner, both, diagonal = (
             (own_ref[rows, :] + other_ref[rows, :]) * (1.0 / 4096.0)
@@ -103,21 +94,16 @@
         damped = _unpack(corner, both, diagonal) + jnp.where(on, 0.1 * total / (members * ORDER), 0.0)
         scaled = 2.5 / jnp.sqrt(jnp.sum(damped * damped, axis=(0, 1), keepdims=True))
         coupled.append(scaled * damped)
-        factor.append(_factor(on, coupled[k]))
-        first_ref[k] = jnp.sqrt(jnp.sqrt(scaled)) * factor[k]
+        first_ref[k] = jnp.sqrt(jnp.sqrt(scaled)) * (jnp.where(on, 1.25, 0.0) - 0.25 * coupled[k])
         current.append(jnp.concatenate([first_ref[k, pl.ds(q * 64 + side * 32, 32), :] for q in range(4)], 0))
-    for step in range(ITERS - 1):
-        if step < FULL_STEPS:
-            square = [_full(factor[k], factor[k]) for k in pair]
-            fourth = [_full(square[k], square[k]) for k in pair]
-            coupled = [_full(fourth[k], coupled[k]) for k in pair]
-        else:
-            parts = [_split(factor[k]) for k in pair]
-            square = [_split(_product(parts[k], parts[k])) for k in pair]
-            fourth = [_split(_product(square[k], square[k])) for k in pair]
-            coupled = [_product(fourth[k], _split(coupled[k])) for k in pair]
-        factor = [_factor(on, coupled[k]) for k in pair]
-        current = [_product(_split(current[k]), _split(factor[k])) for k in pair]
+    parts = [_split(coupled[k]) for k in pair]
+    for _ in range(ITERS - 1):
+        once = [0.0625 * _product(parts[k], parts[k]) - 0.625 * coupled[k] for k in pair]
+        split = [_split(once[k]) for k in pair]
+        twice = [_split(3.125 * once[k] + _product(split[k], split[k])) for k in pair]
+        coupled = [2.44140625 * coupled[k] + _product(twice[k], parts[k]) for k in pair]
+        parts = [_split(coupled[k]) for k in pair]
+        current = [1.25 * current[k] - 0.25 * _product(_split(current[k]), parts[k]) for k in pair]
     for k in pair:
         for c in range(2):
             for q in range(4):

time: 96 us -> 95.3 us (level)
  no operation moved by 1% of the time
where the time goes in v5:
time: 95.3 us; the launch traced here: 95 us
  blocking collectives  28.9 us (30%)
  starting transfers between devices  28.4 us (30%)
  waiting for transfers between devices  24.6 us (26%)
  Pallas kernels  9.49 us (10%)
  local copies, waits for them, and re-layouts  3.28 us (3%)
    all_to_all x1, waiting for transfers between devices, local(): lax.all_to_all(row, ('zh', 'zl', 'x'), 0, 0, tiled=True).reshape(64, HALF)  22.3 us
    all_to_all x1, blocking collectives, local(): pieces = lax.all_to_all(chip, 'y', 0, 0, tiled=True)  17.4 us
    all_to_all x1, blocking collectives, local(): back = lax.all_to_all(rows, ('c', 'y'), 0, 0, tiled=True)  11.5 us
    ppermute x1, starting transfers between devices, local(): other = lax.ppermute(mine, 'zh', [(0, 1), (1, 0)])  11.4 us
    ppermute x1, starting transfers between devices, local(): got = lax.ppermute(send, 'c', [(0, 1), (1, 0)])  8.74 us
    pallas_call x1, Pallas kernels, local(): pl.pallas_call(_solve_kernel, out_shape=jax.ShapeDtypeStruct((8, half //...  8.41 us
    all_to_all x1, starting transfers between devices, local(): lax.all_to_all(row, ('zh', 'zl', 'x'), 0, 0, tiled=True).reshape(64, HALF)  8.21 us
    unnamed x5, local copies, waits for them, and re-layouts  2.3 us
  transfers between devices with their start and end apart: 3, of which 2 were waited for; matrix products, arithmetic and copies ran while one was open for 1% of the time, Pallas kernels for 0%

profile of v5, /device:TPU:1, one launch (start us, length us, event | category | flops | bytes accessed | tf_op | source)
XLA Modules:
  0.0 95.0 jit_solution(9660105283691853124)
XLA Ops:
  0.0 0.0 copy-start
  0.0 1.6 %copy-done = bf16[1,16,1,256,256]{4,3,2,1,0:T(8,128)(2,1)S(1)} copy-done((bf16[1,16,1,256,256]{4,3,2,1,0:T(8,128)(2,1)S(1)}, bf16[1,16,1,256,256]{4,3,2,1,0:T(8,128)(2,1)}, u32[]{:S(2)}) %copy-start) | copy-done | bytes 2097176
  1.6 1.1 %stats.1 = (f32[4,520,128]{2,1,0:T(8,128)S(1)}, f32[4,520,128]{2,1,0:T(8,128)S(1)}) custom-call(s32[1]{0:T(128)} %bitcast.3.where_ref, bf16[16,256,256]{2,1,0:T(8,128)(2,1)S(1)} %bitcast.11), custom_call_target="tpu_custom_call" | custom-call | tf_op jit(solution)/shard_map/stats/pallas_call | solution.py:127
  2.7 8.7 %collective-permute-start = (f32[4,520,128]{2,1,0:T(8,128)S(1)}, f32[4,520,128]{2,1,0:T(8,128)S(1)}, u32[]{:S(2)}, u32[]{:S(2)}) collective-permute-start(f32[4,520,128]{2,1,0:T(8,128)S(1)} %get-tuple-element.8), channel_id=1, source_target_pairs={{0,32},{32,0},{1,33},{33,1},{2,34},{34,2},{3,35},{35,3},{4,36},{36... | collective-permute-start | bytes 3194888 | tf_op jit(solution)/shard_map/ppermute | solution.py:135
  11.4 2.3 %collective-permute-done = f32[4,520,128]{2,1,0:T(8,128)S(1)} collective-permute-done((f32[4,520,128]{2,1,0:T(8,128)S(1)}, f32[4,520,128]{2,1,0:T(8,128)S(1)}, u32[]{:S(2)}, u32[]{:S(2)}) %collective-permute-start) | collective-permute-done | bytes 1064992 | tf_op jit(solution)/shard_map/ppermute | solution.py:135
  13.7 0.1 add.21
  13.8 17.4 %all_to_all.15 = f32[4,520,128]{2,1,0:T(8,128)S(1)} all-to-all(f32[4,520,128]{2,1,0:T(8,128)S(1)} %add.21), channel_id=1, replica_groups=mesh['y'=4,'zh'=2,'c'=2,'zl'=8,'x'=4] {'y'}, dimensions={0} | all-to-all | bytes 2129920 | tf_op jit(solution)/shard_map/all_to_all | solution.py:137
  31.2 0.0 copy-start.1
  31.2 0.1 reduce_sum.9.own_ref
  31.3 11.4 %collective-permute-start.1 = (f32[520,128]{1,0:T(8,128)S(1)}, f32[520,128]{1,0:T(8,128)S(1)}, u32[]{:S(2)}, u32[]{:S(2)}) collective-permute-start(f32[520,128]{1,0:T(8,128)S(1)} %reduce_sum.9.own_ref), channel_id=1, source_target_pairs={{0,64},{64,0},{1,65},{65,1},{2,66},{66,2},{3,67},{67,3},{4,68},{68... | collective-permute-start | bytes 798728 | tf_op jit(solution)/shard_map/ppermute | solution.py:139
  42.7 0.6 broadcast_in_dim.8
  43.3 8.2 %all-to-all-start.1 = ((f32[64,1,128]{2,1,0:T(1,128)}), f32[64,1,128]{2,1,0:T(1,128)S(1)}, u32[]{:S(2)}, u32[]{:S(2)}) async-start(f32[64,1,128]{2,1,0:T(1,128)} %broadcast_in_dim.8), calls=%async_computation.1 | async-start | bytes 65536 | tf_op jit(solution)/shard_map/all_to_all | solution.py:141
  51.6 0.0 copy-done.1
  51.6 0.1 reshape.26
  51.7 0.1 copy.8
  51.7 0.2 dynamic-slice_reduce_fusion
  52.0 0.1 pad_add_fusion.where_ref
  52.0 22.3 %all-to-all-done.1 = f32[64,1,128]{2,1,0:T(1,128)S(1)} async-done(((f32[64,1,128]{2,1,0:T(1,128)}), f32[64,1,128]{2,1,0:T(1,128)S(1)}, u32[]{:S(2)}, u32[]{:S(2)}) %all-to-all-start.1) | async-done | bytes 32800 | tf_op jit(solution)/shard_map/all_to_all | solution.py:141
  74.3 0.0 collective-permute-done.1.other_ref
  74.3 8.4 %solve.1 = f32[8,2,16,256]{3,2,1,0:T(8,128)S(1)} custom-call(s32[3]{0:T(128)S(1)} %pad_add_fusion.where_ref, s32[64,128]{1,0:T(8,128)S(1)} %pad.4.map_ref, f32[520,128]{1,0:T(8,128)S(1)} %reduce_sum.9.own_ref, f32[520,128]{1,0:T(8,128)S(1)} %collective-permute-done.1.other_ref, f32[64,128]{1,0:T(8,128)S(1)} %bitcast.12), custom_call_target="tpu_custom_call" | custom-call | tf_op jit(solution)/shard_map/solve/pallas_call | solution.py:146
  82.8 11.5 %all_to_all.16 = f32[8,2,16,256]{3,2,1,0:T(8,128)S(1)} all-to-all(f32[8,2,16,256]{3,2,1,0:T(8,128)S(1)} %solve.1), channel_id=1, replica_groups=mesh['y'=4,'zh'=2,'c'=2,'zl'=8,'x'=4] {'c','y'}, dimensions={0} | all-to-all | bytes 524288 | tf_op jit(solution)/shard_map/all_to_all | solution.py:155
  94.3 0.7 copy.11
  (3 shorter events, 0.0 us)
Async XLA Ops:
  0.0 1.6 %copy-start = (bf16[1,16,1,256,256]{4,3,2,1,0:T(8,128)(2,1)S(1)}, bf16[1,16,1,256,256]{4,3,2,1,0:T(8,128)(2,1)}, u32[]{:S(2)}) copy-start(bf16[1,16,1,256,256]{4,3,2,1,0:T(8,128)(2,1)} %param.2) | copy-start | bytes 6291460
  2.7 11.0 %collective-permute-start = (f32[4,520,128]{2,1,0:T(8,128)S(1)}, f32[4,520,128]{2,1,0:T(8,128)S(1)}, u32[]{:S(2)}, u32[]{:S(2)}) collective-permute-start(f32[4,520,128]{2,1,0:T(8,128)S(1)} %get-tuple-element.8), channel_id=1, source_target_pairs={{0,32},{32,0},{1,33},{33,1},{2,34},{34,2},{3,35},{35,3},{4,36},{36... | collective-permute-start | bytes 3194888 | tf_op jit(solution)/shard_map/ppermute | solution.py:135
  31.2 20.4 %copy-start.1 = (s32[512]{0:T(512)S(1)}, s32[512]{0:T(512)}, u32[]{:S(2)}) copy-start(s32[512]{0:T(512)} %param.3) | copy-start | bytes 6148
  31.3 43.0 %collective-permute-start.1 = (f32[520,128]{1,0:T(8,128)S(1)}, f32[520,128]{1,0:T(8,128)S(1)}, u32[]{:S(2)}, u32[]{:S(2)}) collective-permute-start(f32[520,128]{1,0:T(8,128)S(1)} %reduce_sum.9.own_ref), channel_id=1, source_target_pairs={{0,64},{64,0},{1,65},{65,1},{2,66},{66,2},{3,67},{67,3},{4,68},{68... | collective-permute-start | bytes 798728 | tf_op jit(solution)/shard_map/ppermute | solution.py:139
  43.3 31.0 %all-to-all-start.1 = ((f32[64,1,128]{2,1,0:T(1,128)}), f32[64,1,128]{2,1,0:T(1,128)S(1)}, u32[]{:S(2)}, u32[]{:S(2)}) async-start(f32[64,1,128]{2,1,0:T(1,128)} %broadcast_in_dim.8), calls=%async_computation.1 | async-start | bytes 65536 | tf_op jit(solution)/shard_map/all_to_all | solution.py:141

commit v6 on v5

--- a/solution.py
+++ b/solution.py
@@ -5,6 +5,7 @@
 from jax.experimental.pallas import tpu as pltpu
 from jax.sharding import Mesh
 from jax.sharding import PartitionSpec as P
+
 
 ITERS = 8
 ORDER = 256
@@ -73,13 +74,11 @@
     return jnp.concatenate([jnp.concatenate([left, corner], 1), jnp.concatenate([corner.T, low], 1)], 0)
 
 
-def _solve_kernel(where_ref, map_ref, own_ref, other_ref, traces_ref, out_ref, first_ref):
-    side = where_ref[0]
-    pair = range(2)
+def _prepare_kernel(own_ref, other_ref, stats_ref, square_ref, norms_ref):
     row, col = _iotas((ORDER, ORDER))
-    on = row == col
-    coupled, current = [], []
-    for k in pair:
+    norm_row, _ = _iotas((8, HALF))
+    norms = jnp.zeros((8, HALF), jnp.float32)
+    for k in range(2):
         corner, both, diagonal = (
             (own_ref[rows, :] + other_ref[rows, :]) * (1.0 / 4096.0)
             for rows in (
@@ -88,17 +87,37 @@
                 slice(TAIL + k, TAIL + k + 1),
             )
         )
+        stats = _unpack(corner, both, diagonal)
+        parts = _split(stats)
+        stats_ref[k] = stats
+        square_ref[k] = _product(parts, parts)
+        norms = jnp.where(norm_row == k, jnp.sum(stats * stats, axis=(0, 1), keepdims=True), norms)
+        norms = jnp.where(norm_row == 2 + k, jnp.sum(jnp.where(row == col, stats, 0.0), axis=(0, 1), keepdims=True), norms)
+    norms_ref[...] = norms
+
+
+def _solve_kernel(where_ref, map_ref, stats_ref, square_ref, norms_ref, traces_ref, out_ref, first_ref):
+    side = where_ref[0]
+    pair = range(2)
+    row, col = _iotas((ORDER, ORDER))
+    on = row == col
+    coupled, current, once = [], [], []
+    for k in pair:
         held = map_ref[...] == where_ref[1 + k]
         members = jnp.sum(jnp.where(held, 0.5, 0.0), axis=(0, 1), keepdims=True)
         total = jnp.sum(jnp.where(held, traces_ref[...], 0.0), axis=(0, 1), keepdims=True) * (1.0 / 4096.0)
-        damped = _unpack(corner, both, diagonal) + jnp.where(on, 0.1 * total / (members * ORDER), 0.0)
-        scaled = 2.5 / jnp.sqrt(jnp.sum(damped * damped, axis=(0, 1), keepdims=True))
-        coupled.append(scaled * damped)
+        ridge = 0.1 * total / (members * ORDER)
+        squares = norms_ref[k : k + 1, 0:1] + ridge * (2.0 * norms_ref[2 + k : 3 + k, 0:1] + ORDER * ridge)
+        scaled = 2.5 / jnp.sqrt(squares)
+        coupled.append(scaled * (stats_ref[k] + jnp.where(on, ridge, 0.0)))
         first_ref[k] = jnp.sqrt(jnp.sqrt(scaled)) * (jnp.where(on, 1.25, 0.0) - 0.25 * coupled[k])
+        square = (scaled * scaled) * (square_ref[k] + ((2.0 * ridge) * stats_ref[k] + jnp.where(on, ridge * ridge, 0.0)))
+        once.append(0.0625 * square - 0.625 * coupled[k])
         current.append(jnp.concatenate([first_ref[k, pl.ds(q * 64 + side * 32, 32), :] for q in range(4)], 0))
     parts = [_split(coupled[k]) for k in pair]
-    for _ in range(ITERS - 1):
-        once = [0.0625 * _product(parts[k], parts[k]) - 0.625 * coupled[k] for k in pair]
+    for step in range(ITERS - 1):
+        if step > 0:
+            once = [0.0625 * _product(parts[k], parts[k]) - 0.625 * coupled[k] for k in pair]
         split = [_split(once[k]) for k in pair]
         twice = [_split(3.125 * once[k] + _product(split[k], split[k])) for k in pair]
         coupled = [2.44140625 * coupled[k] + _product(twice[k], parts[k]) for k in pair]
@@ -143,15 +162,24 @@
     layer_of = jnp.pad(jnp.tile(layers.T, (2, 1)), ((0, 0), (0, HALF - 2 * half)), constant_values=-1)
     block = core * half + line * 2
     pair = lax.dynamic_slice(layers, (block, holder), (2, 1)).reshape(2)
+    whole = jax.ShapeDtypeStruct((half // 4, ORDER, ORDER), jnp.float32)
+    prepared = pl.pallas_call(
+        _prepare_kernel,
+        out_shape=(whole, whole, jax.ShapeDtypeStruct((8, HALF), jnp.float32)),
+        in_specs=[_vmem()] * 2,
+        out_specs=(_vmem(),) * 3,
+        compiler_params=pltpu.CompilerParams(vmem_limit_bytes=16 * 2**20),
+        name="prepare",
+    )(mine, other)
     rows = pl.pallas_call(
         _solve_kernel,
         out_shape=jax.ShapeDtypeStruct((8, half // 4, 16, ORDER), jnp.float32),
-        in_specs=[_smem()] + [_vmem()] * 4,
+        in_specs=[_smem()] + [_vmem()] * 5,
         out_specs=_vmem(),
         scratch_shapes=[pltpu.VMEM((half // 4, ORDER, ORDER), jnp.float32)],
         compiler_params=pltpu.CompilerParams(vmem_limit_bytes=16 * 2**20),
         name="solve",
-    )(jnp.concatenate([side.astype(jnp.int32).reshape(1), pair]), layer_of, mine, other, traces)
+    )(jnp.concatenate([side.astype(jnp.int32).reshape(1), pair]), layer_of, *prepared, traces)
     back = lax.all_to_all(rows, ("c", "y"), 0, 0, tiled=True)
     return back.reshape(16, 1, 16, ORDER)
 

time: 95.3 us -> 94.7 us (level)
  transfers between devices with their start and end apart: 3 -> 3, of which waited for: 2 -> 2; matrix products, arithmetic and copies ran while one was open for 1% -> 1% of each run, Pallas kernels for 0% -> 1%
where the time goes in v6:
time: 94.7 us; the launch traced here: 94.4 us
  blocking collectives  28.9 us (31%)
  starting transfers between devices  28.4 us (30%)
  waiting for transfers between devices  24 us (25%)
  Pallas kernels  9.46 us (10%)
  local copies, waits for them, and re-layouts  3.28 us (3%)
    all_to_all x1, waiting for transfers between devices, local(): lax.all_to_all(row, ('zh', 'zl', 'x'), 0, 0, tiled=True).reshape(64, HALF)  21.7 us
    all_to_all x1, blocking collectives, local(): pieces = lax.all_to_all(chip, 'y', 0, 0, tiled=True)  17.4 us
    all_to_all x1, blocking collectives, local(): back = lax.all_to_all(rows, ('c', 'y'), 0, 0, tiled=True)  11.5 us
    ppermute x1, starting transfers between devices, local(): other = lax.ppermute(mine, 'zh', [(0, 1), (1, 0)])  11.4 us
    ppermute x1, starting transfers between devices, local(): got = lax.ppermute(send, 'c', [(0, 1), (1, 0)])  8.74 us
    all_to_all x1, starting transfers between devices, local(): lax.all_to_all(row, ('zh', 'zl', 'x'), 0, 0, tiled=True).reshape(64, HALF)  8.21 us
    pallas_call x1, Pallas kernels, local(): pl.pallas_call(_solve_kernel, out_shape=jax.ShapeDtypeStruct((8, half //...  7.84 us
    unnamed x5, local copies, waits for them, and re-layouts  2.3 us
  transfers between devices with their start and end apart: 3, of which 2 were waited for; matrix products, arithmetic and copies ran while one was open for 1% of the time, Pallas kernels for 1%

profile of v6, /device:TPU:1, one launch (start us, length us, event | category | flops | bytes accessed | tf_op | source)
XLA Modules:
  0.0 94.4 jit_solution(16903018385218690107)
XLA Ops:
  0.0 0.0 copy-start
  0.0 1.6 %copy-done = bf16[1,16,1,256,256]{4,3,2,1,0:T(8,128)(2,1)S(1)} copy-done((bf16[1,16,1,256,256]{4,3,2,1,0:T(8,128)(2,1)S(1)}, bf16[1,16,1,256,256]{4,3,2,1,0:T(8,128)(2,1)}, u32[]{:S(2)}) %copy-start) | copy-done | bytes 2097176
  1.6 1.1 %stats.1 = (f32[4,520,128]{2,1,0:T(8,128)S(1)}, f32[4,520,128]{2,1,0:T(8,128)S(1)}) custom-call(s32[1]{0:T(128)} %bitcast.3.where_ref, bf16[16,256,256]{2,1,0:T(8,128)(2,1)S(1)} %bitcast.11), custom_call_target="tpu_custom_call" | custom-call | tf_op jit(solution)/shard_map/stats/pallas_call | solution.py:146
  2.7 8.7 %collective-permute-start = (f32[4,520,128]{2,1,0:T(8,128)S(1)}, f32[4,520,128]{2,1,0:T(8,128)S(1)}, u32[]{:S(2)}, u32[]{:S(2)}) collective-permute-start(f32[4,520,128]{2,1,0:T(8,128)S(1)} %get-tuple-element.11), channel_id=1, source_target_pairs={{0,32},{32,0},{1,33},{33,1},{2,34},{34,2},{3,35},{35,3},{4,36},{36... | collective-permute-start | bytes 3194888 | tf_op jit(solution)/shard_map/ppermute | solution.py:154
  11.4 2.3 %collective-permute-done = f32[4,520,128]{2,1,0:T(8,128)S(1)} collective-permute-done((f32[4,520,128]{2,1,0:T(8,128)S(1)}, f32[4,520,128]{2,1,0:T(8,128)S(1)}, u32[]{:S(2)}, u32[]{:S(2)}) %collective-permute-start) | collective-permute-done | bytes 1064992 | tf_op jit(solution)/shard_map/ppermute | solution.py:154
  13.7 0.1 add.21
  13.8 17.4 %all_to_all.15 = f32[4,520,128]{2,1,0:T(8,128)S(1)} all-to-all(f32[4,520,128]{2,1,0:T(8,128)S(1)} %add.21), channel_id=1, replica_groups=mesh['y'=4,'zh'=2,'c'=2,'zl'=8,'x'=4] {'y'}, dimensions={0} | all-to-all | bytes 2129920 | tf_op jit(solution)/shard_map/all_to_all | solution.py:156
  31.2 0.0 copy-start.1
  31.2 0.1 reduce_sum.9.own_ref
  31.3 11.4 %collective-permute-start.1 = (f32[520,128]{1,0:T(8,128)S(1)}, f32[520,128]{1,0:T(8,128)S(1)}, u32[]{:S(2)}, u32[]{:S(2)}) collective-permute-start(f32[520,128]{1,0:T(8,128)S(1)} %reduce_sum.9.own_ref), channel_id=1, source_target_pairs={{0,64},{64,0},{1,65},{65,1},{2,66},{66,2},{3,67},{67,3},{4,68},{68... | collective-permute-start | bytes 798728 | tf_op jit(solution)/shard_map/ppermute | solution.py:158
  42.7 0.6 broadcast_in_dim.8
  43.3 8.2 %all-to-all-start.1 = ((f32[64,1,128]{2,1,0:T(1,128)}), f32[64,1,128]{2,1,0:T(1,128)S(1)}, u32[]{:S(2)}, u32[]{:S(2)}) async-start(f32[64,1,128]{2,1,0:T(1,128)} %broadcast_in_dim.8), calls=%async_computation.1 | async-start | bytes 65536 | tf_op jit(solution)/shard_map/all_to_all | solution.py:160
  51.6 0.0 copy-done.1
  51.6 0.1 reshape.26
  51.7 0.1 copy.8
  51.7 0.2 dynamic-slice_reduce_fusion
  52.0 0.1 pad_add_fusion.where_ref
  52.0 0.0 collective-permute-done.1.other_ref
  52.0 0.5 prepare.1
  52.6 21.7 %all-to-all-done.1 = f32[64,1,128]{2,1,0:T(1,128)S(1)} async-done(((f32[64,1,128]{2,1,0:T(1,128)}), f32[64,1,128]{2,1,0:T(1,128)S(1)}, u32[]{:S(2)}, u32[]{:S(2)}) %all-to-all-start.1) | async-done | bytes 32800 | tf_op jit(solution)/shard_map/all_to_all | solution.py:160
  74.3 7.8 %solve.1 = f32[8,2,16,256]{3,2,1,0:T(8,128)S(1)} custom-call(s32[3]{0:T(128)S(1)} %pad_add_fusion.where_ref, s32[64,128]{1,0:T(8,128)S(1)} %pad.4.map_ref, f32[2,256,256]{2,1,0:T(8,128)S(1)} %get-tuple-element.12.stats_ref, f32[2,256,256]{2,1,0:T(8,128)S(1)} %get-tuple-element.13.square_ref, f32[8,128]{1,0:T(8,128)S(1)} %get-tuple-element.14.norms_ref, ...), custom_call_target="tpu_custom_call" | custom-call | tf_op jit(solution)/shard_map/solve/pallas_call | solution.py:174
  82.2 11.5 %all_to_all.16 = f32[8,2,16,256]{3,2,1,0:T(8,128)S(1)} all-to-all(f32[8,2,16,256]{3,2,1,0:T(8,128)S(1)} %solve.1), channel_id=1, replica_groups=mesh['y'=4,'zh'=2,'c'=2,'zl'=8,'x'=4] {'c','y'}, dimensions={0} | all-to-all | bytes 524288 | tf_op jit(solution)/shard_map/all_to_all | solution.py:183
  93.7 0.7 copy.11
  (3 shorter events, 0.0 us)
Async XLA Ops:
  0.0 1.6 %copy-start = (bf16[1,16,1,256,256]{4,3,2,1,0:T(8,128)(2,1)S(1)}, bf16[1,16,1,256,256]{4,3,2,1,0:T(8,128)(2,1)}, u32[]{:S(2)}) copy-start(bf16[1,16,1,256,256]{4,3,2,1,0:T(8,128)(2,1)} %param.2) | copy-start | bytes 6291460
  2.7 11.0 %collective-permute-start = (f32[4,520,128]{2,1,0:T(8,128)S(1)}, f32[4,520,128]{2,1,0:T(8,128)S(1)}, u32[]{:S(2)}, u32[]{:S(2)}) collective-permute-start(f32[4,520,128]{2,1,0:T(8,128)S(1)} %get-tuple-element.11), channel_id=1, source_target_pairs={{0,32},{32,0},{1,33},{33,1},{2,34},{34,2},{3,35},{35,3},{4,36},{36... | collective-permute-start | bytes 3194888 | tf_op jit(solution)/shard_map/ppermute | solution.py:154
  31.2 20.4 %copy-start.1 = (s32[512]{0:T(512)S(1)}, s32[512]{0:T(512)}, u32[]{:S(2)}) copy-start(s32[512]{0:T(512)} %param.3) | copy-start | bytes 6148
  31.3 20.7 %collective-permute-start.1 = (f32[520,128]{1,0:T(8,128)S(1)}, f32[520,128]{1,0:T(8,128)S(1)}, u32[]{:S(2)}, u32[]{:S(2)}) collective-permute-start(f32[520,128]{1,0:T(8,128)S(1)} %reduce_sum.9.own_ref), channel_id=1, source_target_pairs={{0,64},{64,0},{1,65},{65,1},{2,66},{66,2},{3,67},{67,3},{4,68},{68... | collective-permute-start | bytes 798728 | tf_op jit(solution)/shard_map/ppermute | solution.py:158
  43.3 31.0 %all-to-all-start.1 = ((f32[64,1,128]{2,1,0:T(1,128)}), f32[64,1,128]{2,1,0:T(1,128)S(1)}, u32[]{:S(2)}, u32[]{:S(2)}) async-start(f32[64,1,128]{2,1,0:T(1,128)} %broadcast_in_dim.8), calls=%async_computation.1 | async-start | bytes 65536 | tf_op jit(solution)/shard_map/all_to_all | solution.py:160
